TPU v7x, 32 devices: a whole 2x2x4 slice. The times are simulated.
32 devices in a mesh: dp: 16 (over z, y, x), tensor: 2 (over core).
Axes of the slice: x: 2, y: 2, z: 4, core: 2. Of those that a mesh axis runs over, the one named last changes fastest.
Arguments:
- streams: bfloat16 [2048, 4, 8192], P('dp', None, 'tensor'), may hold values from -6 to 6
- layer_out: bfloat16 [2048, 8192], P('dp', 'tensor'), may hold values from -6 to 6
- cotangent: bfloat16 [2048, 4, 8192], P('dp', None, 'tensor'), may hold values from -6 to 6
- input_cot: bfloat16 [2048, 8192], P('dp', 'tensor'), may hold values from -6 to 6
- gain: float32 [8192], P('tensor'), may hold values from 0.5 to 1.5
- projection: float32 [6, 8192], P(None, 'tensor'), may hold values from -0.0625 to 0.0625
- static_mix: float32 [4, 6], replicated, may hold values from -3 to 3
- tanh_scale: float32 [3], replicated, may hold values from 0.5 to 2
Outputs:
- stream_grad: bfloat16 [2048, 4, 8192], P('dp', None, 'tensor')
- out_grad: bfloat16 [2048, 8192], P('dp', 'tensor')
- proj_grad: float32 [6, 8192], P(None, 'tensor')
- gain_grad: float32 [8192], P('tensor')
All inputs are finite; a program needn't handle non-finite values.
Results may differ from a plain program's by a relative error of at most 0.0018.
Values sent between devices are 32-bit elements; how exact they have to be, the bound alone decides.
No kernel may reach another device: no remote copies, remote signals or barrier semaphores. Data moves between devices by JAX's collectives and lax.ppermute only.
A program may use at most 64 MiB of HBM per device.

v0:
```python
import jax
import jax.numpy as jnp
from jax import lax
from jax.sharding import PartitionSpec as P

D = 8192


def nonlinear(square, lin, dbeta, dalpha, dmixer, static_mix, tanh_scale):
    inv_rms = lax.rsqrt(square / D + 1e-06)
    bent = jnp.tanh(inv_rms[..., None] * lin)
    scales = jnp.concatenate([tanh_scale[0:2], jnp.repeat(tanh_scale[2:3], 4)])
    coef = static_mix[None] + scales * bent
    dcoef = jnp.concatenate([dbeta[..., None], dalpha[..., None], dmixer], axis=-1)
    dpre = dcoef * scales * (1.0 - bent * bent)
    dlin = dpre * inv_rms[..., None]
    dsquare = -0.5 * inv_rms**3 / D * jnp.sum(dpre * lin, axis=-1)
    return (coef, dlin, dsquare)


def shards(streams, layer_out, cotangent, input_cot, gain, projection, static_mix, tanh_scale):
    wproj = gain[None, :] * projection
    square = jnp.einsum("tjd,tjd->tj", streams, streams, preferred_element_type=jnp.float32)
    lin = jnp.stack([jnp.sum(streams * wproj[column], axis=-1) for column in range(6)], axis=-1)
    dbeta = jnp.einsum("td,tkd->tk", layer_out, cotangent, preferred_element_type=jnp.float32)
    dalpha = jnp.einsum("tjd,td->tj", streams, input_cot, preferred_element_type=jnp.float32)
    dmixer = jnp.einsum("tjd,tkd->tjk", streams, cotangent, preferred_element_type=jnp.float32)
    square, lin = lax.psum((square, lin), "tensor")
    dbeta, dalpha, dmixer = lax.psum((dbeta, dalpha, dmixer), "tensor")
    coef, dlin, dsquare = nonlinear(square, lin, dbeta, dalpha, dmixer, static_mix, tanh_scale)
    out_total = coef[:, 0, 0][:, None] * cotangent[:, 0, :]
    for stream in range(1, 4):
        out_total = out_total + coef[:, stream, 0][:, None] * cotangent[:, stream, :]
    out_grad = out_total.astype(jnp.bfloat16)
    total = coef[:, :, 1][..., None] * input_cot[:, None, :]
    for stream in range(4):
        total = total + coef[:, :, 2 + stream][..., None] * cotangent[:, stream, :][:, None, :]
    for column in range(6):
        total = total + dlin[:, :, column][..., None] * wproj[column]
    total = total + (2.0 * dsquare)[..., None] * streams
    stream_grad = total.astype(jnp.bfloat16)
    dweight = jnp.stack(
        [jnp.sum(dlin[:, :, column][..., None] * streams, axis=(0, 1)) for column in range(6)],
        axis=0,
    )
    proj_part = gain[None, :] * dweight
    gain_part = jnp.sum(dweight * projection, axis=0)
    proj_sum, gain_sum = lax.psum((proj_part, gain_part), "dp")
    all_tokens = streams.shape[0] * lax.axis_size("dp")
    proj_grad = proj_sum / jnp.sqrt(4.0 * all_tokens * D)
    gain_grad = gain_sum / jnp.sqrt(4.0 * all_tokens)
    return (stream_grad, out_grad, proj_grad, gain_grad)


def solution(mesh):
    placed = (
        P("dp", None, "tensor"),
        P("dp", "tensor"),
        P("dp", None, "tensor"),
        P("dp", "tensor"),
        P("tensor"),
        P(None, "tensor"),
        P(),
        P(),
    )
    return jax.shard_map(
        shards,
        mesh=mesh,
        in_specs=placed,
        out_specs=(P("dp", None, "tensor"), P("dp", "tensor"), P(None, "tensor"), P("tensor")),
        check_vma=False,
    )
```

profile of v0, /device:TPU:0, one launch (start us, length us, event | category | flops | bytes accessed | tf_op | source)
XLA Modules:
  0.0 221.9 jit_solution(14247257589624999736)
XLA Ops:
  7.2 0.9 broadcast_multiply_fusion.2
  8.1 0.1 fusion.29
  8.3 15.9 %fusion = (f32[128,4]{1,0:T(8,128)S(1)}, f32[128,4]{1,0:T(8,128)S(1)}, f32[128,4]{1,0:T(8,128)S(1)}, f32[128,4]{1,0:T(8,128)S(1)}, f32[128,4]{1,0:T(8,128)S(1)}, /*index=5*/f32[128,4]{1,0:T(8,128)S(1)}, f32[128,4]{1,0:T(8,128)S(1)}) fusion(bf16[128,4,4096]{2,1,0:T(4,128)(2,1)} %param.8, f32[4096]{0:T(1024)S(1)} %bitcast.105, f32[4096]{0:T(1024)S(1)} %bitcast.103, ...), kind=kLoop, calls=%fused_computation.14 | loop fusion | flops 31453696 | bytes 4306944
  24.2 0.1 copy.51
  24.3 0.1 copy.52
  24.4 0.1 copy.53
  24.4 0.1 copy.54
  24.5 0.1 copy.55
  24.6 0.1 copy.56
  24.8 9.0 %fusion.30 = f32[128,4,4]{2,1,0:T(4,128)S(1)} fusion(bf16[128,4,4096]{2,1,0:T(4,128)(2,1)} %param.8, bf16[128,4,4096]{2,1,0:T(4,128)(2,1)} %param.10), kind=kOutput, calls=%fused_computation.81 | convolution fusion | flops 16777216 | bytes 8396800 | tf_op jit(solution)/shard_map/tjd,tkd->tjk/dot_general | solution.py:27
  33.9 5.5 %fusion.17 = f32[128,1,4]{2,1,0:T(1,128)S(1)} fusion(bf16[128,4,4096]{2,1,0:T(4,128)(2,1)S(1)} %copy-done.4, bf16[128,4096,1]{1,0,2:T(8,128)(2,1)S(1)} %bitcast.115), kind=kOutput, calls=%fused_computation.32 | convolution fusion | flops 4194304 | bytes 5244928 | tf_op jit(solution)/shard_map/td,tkd->tk/dot_general | solution.py:25
  39.4 0.1 copy.79
  39.5 7.7 %fusion.15 = f32[128,1,4]{2,1,0:T(1,128)S(1)} fusion(bf16[128,4,4096]{2,1,0:T(4,128)(2,1)} %param.8, bf16[128,4096,1]{1,0,2:T(8,128)(2,1)S(1)} %bitcast.94), kind=kOutput, calls=%fused_computation.30 | convolution fusion | flops 4194304 | bytes 5244928 | tf_op jit(solution)/shard_map/tjd,td->tj/dot_general | solution.py:26
  47.2 0.1 copy.81
  47.4 4.4 %all-reduce.1 = (f32[128,4,4]{2,1,0:T(4,128)S(1)}, f32[128,4,1]{0,1,2:T(4,128)S(1)}, f32[128,4,1]{0,1,2:T(4,128)S(1)}, f32[128,4,6]{0,1,2:T(4,128)S(1)}, f32[128,4]{0,1:T(4,128)S(1)}) all-reduce(f32[128,4,4]{2,1,0:T(4,128)S(1)} %fusion.30, f32[128,4,1]{0,1,2:T(4,128)S(1)} %bitcast.114, ...), channel_id=1, replica_groups=mesh['dp'=16,'tensor'=2] {'tensor'}, use_global_device_ids=true, to_apply=%region_10.0 | all-reduce | flops 6656 | bytes 53248 | tf_op jit(solution)/shard_map/psum | solution.py:29
  51.8 0.1 copy.66
  51.9 0.1 copy.50
  52.0 0.6 slice.100
  52.6 0.6 concatenate.6
  53.3 0.7 broadcast_multiply_fusion.4
  53.9 0.6 slice_bitcast_fusion.5
  54.5 0.1 copy.67
  54.6 0.1 copy.68
  54.7 0.1 copy.69
  54.9 0.1 copy.70
  55.0 0.1 copy.71
  55.1 0.1 copy.72
  55.2 13.4 %fusion.14 = (f32[4096]{0:T(1024)S(1)}, f32[4096]{0:T(1024)S(1)}, f32[4096]{0:T(1024)S(1)}, f32[4096]{0:T(1024)S(1)}, f32[4096]{0:T(1024)S(1)}, /*index=5*/f32[4096]{0:T(1024)S(1)}) fusion(bf16[128,4,4096]{2,1,0:T(4,128)(2,1)} %param.8, f32[128,4]{1,0:T(8,128)S(1)} %copy.72, f32[128,4]{1,0:T(8,128)S(1)} %copy.67, f32[128,4]{1,0:T(8,128)S(1)} %copy.68, ...), kind=kLoop, calls=%fused_computation.28 | loop fusion | flops 27238400 | bytes 4304896 | tf_op jit(solution)/shard_map/reduce_sum | solution.py:43
  68.6 0.2 stack.55
  68.7 1.3 multiply_reduce_fusion
  70.1 0.6 slice_bitcast_fusion.14
  70.7 16.2 %fusion.28 = (bf16[128,1,4096]{2,1,0:T(2,128)(2,1)S(1)}, bf16[128,1,4096]{2,1,0:T(2,128)(2,1)}, bf16[128,1,4096]{2,1,0:T(2,128)(2,1)}, bf16[128,1,4096]{2,1,0:T(2,128)(2,1)}) fusion(bf16[128,4,4096]{2,1,0:T(4,128)(2,1)} %param.10), kind=kLoop, calls=%fused_computation.79 | loop fusion | bytes 8388608 | tf_op jit(solution)/shard_map/slice | solution.py:37
  86.8 1.6 convert_element_type.14
  88.4 78.2 %psum.55 = f32[4096]{0:T(1024)S(1)} all-reduce(f32[4096]{0:T(1024)} %get-tuple-element.28), channel_id=1, replica_groups=mesh['dp'=16,'tensor'=2] {'dp'}, use_global_device_ids=true, to_apply=%region_20.0 | all-reduce | flops 4096 | bytes 32768 | tf_op jit(solution)/shard_map/psum | solution.py:48
  166.6 0.7 copy.57
  167.3 0.8 copy.58
  168.1 0.8 copy.60
  168.9 0.8 copy.62
  169.6 0.8 copy.64
  170.4 0.7 multiply_reduce_fusion.1
  171.1 0.7 fusion.26
  171.8 0.1 copy.73
  172.0 5.6 %fusion.21 = (f32[128,4096]{1,0:T(8,128)S(1)}, f32[128,4096]{1,0:T(8,128)S(1)}) fusion(bf16[128,1,4096]{2,1,0:T(2,128)(2,1)} %get-tuple-element.26, bf16[128,1,4096]{2,1,0:T(2,128)(2,1)S(1)} %get-tuple-element.24), kind=kLoop, calls=%fused_computation.39 | loop fusion | flops 1048576 | bytes 6291456 | tf_op jit(solution)/shard_map/mul | solution.py:37
  177.6 3.9 %fusion.19 = (f32[128,4096]{1,0:T(8,128)S(1)}, f32[128,4096]{1,0:T(8,128)S(1)}) fusion(bf16[128,1,4096]{2,1,0:T(2,128)(2,1)S(1)} %copy-done.3, bf16[128,1,4096]{2,1,0:T(2,128)(2,1)S(1)} %copy-done.1), kind=kLoop, calls=%fused_computation.35 | loop fusion | flops 1048576 | bytes 6291456 | tf_op jit(solution)/shard_map/mul | solution.py:37
  181.6 9.8 %add_convert_fusion = bf16[128,4096]{1,0:T(8,128)(2,1)} fusion(f32[128]{0:T(128)S(1)} %copy-done.22, f32[128]{0:T(128)S(1)} %copy-done.23, f32[128]{0:T(128)S(1)} %copy-done.24, f32[128]{0:T(128)S(1)} %copy-done.21, bf16[128,1,4096]{2,1,0:T(2,128)(2,1)S(1)} %get-tuple-element.24, bf16[128,1,4096]{2,1,0:T(2,128)(2,1)S(1)} %copy-done.2, ...), kind=kLoop, calls=%fused_computation.29 | loop fusion | flops 6291456 | bytes 5244928 | tf_op jit(solution)/shard_map/convert_element_type | solution.py:34
  191.5 20.9 %fusion.8 = bf16[128,4,4096]{2,1,0:T(4,128)(2,1)} fusion(bf16[128,4,4096]{2,1,0:T(4,128)(2,1)S(1)} %copy-done, f32[128,4]{1,0:T(8,128)S(1)} %copy.73, f32[128,4]{1,0:T(8,128)S(1)} %copy.72, f32[128,4]{1,0:T(8,128)S(1)} %copy.71, f32[128,4]{1,0:T(8,128)S(1)} %copy.70, f32[128,4]{1,0:T(8,128)S(1)} %copy.69, f32[128,4]{1,0:T(8,128)S(1)} %copy.68, ...), kind=kLoop, calls=%fused_computation.22 | loop fusion | flops 52428800 | bytes 18997248 | tf_op jit(solution)/shard_map/convert_element_type | solution.py:41
  212.4 0.6 broadcast_multiply_fusion.3
  213.1 1.6 broadcast_multiply_fusion
  (67 shorter events, 0.4 us)
Async XLA Ops:
  7.2 205.9 %all-reduce.4.cloned.1.call-start = ((), (), s32[]{:S(2)}) async-start(), calls=%async_computation | async-start | bytes 262144 | tf_op jit(solution)/shard_map/psum | solution.py:48
  8.2 16.5 %copy-start.8 = (f32[1,4096]{1,0:T(1,128)}, f32[1,4096]{1,0:T(1,128)S(1)}, u32[]{:S(2)}) copy-start(f32[1,4096]{1,0:T(1,128)S(1)} %get-tuple-element.31) | copy-start | bytes 49156
  8.2 16.4 %copy-start.10 = (f32[1,4096]{1,0:T(1,128)}, f32[1,4096]{1,0:T(1,128)S(1)}, u32[]{:S(2)}) copy-start(f32[1,4096]{1,0:T(1,128)S(1)} %get-tuple-element.32) | copy-start | bytes 49156
  8.2 16.5 %copy-start.12 = (f32[1,4096]{1,0:T(1,128)}, f32[1,4096]{1,0:T(1,128)S(1)}, u32[]{:S(2)}) copy-start(f32[1,4096]{1,0:T(1,128)S(1)} %get-tuple-element.33) | copy-start | bytes 49156
  8.2 16.5 %copy-start.14 = (f32[1,4096]{1,0:T(1,128)}, f32[1,4096]{1,0:T(1,128)S(1)}, u32[]{:S(2)}) copy-start(f32[1,4096]{1,0:T(1,128)S(1)} %get-tuple-element.34) | copy-start | bytes 49156
  8.3 25.6 %copy-start.16 = (f32[1,4096]{1,0:T(1,128)}, f32[1,4096]{1,0:T(1,128)S(1)}, u32[]{:S(2)}) copy-start(f32[1,4096]{1,0:T(1,128)S(1)} %get-tuple-element.35) | copy-start | bytes 49156
  24.8 9.1 %copy-start.4 = (bf16[128,4,4096]{2,1,0:T(4,128)(2,1)S(1)}, bf16[128,4,4096]{2,1,0:T(4,128)(2,1)}, u32[]{:S(2)}) copy-start(bf16[128,4,4096]{2,1,0:T(4,128)(2,1)} %param.10) | copy-start | bytes 12582916
  24.8 9.1 %copy-start.26 = (bf16[128,4096]{1,0:T(8,128)(2,1)S(1)}, bf16[128,4096]{1,0:T(8,128)(2,1)}, u32[]{:S(2)}) copy-start(bf16[128,4096]{1,0:T(8,128)(2,1)} %param.9) | copy-start | bytes 3145732
  33.8 5.6 %copy-start.6 = (bf16[128,4096]{1,0:T(8,128)(2,1)S(1)}, bf16[128,4096]{1,0:T(8,128)(2,1)}, u32[]{:S(2)}) copy-start(bf16[128,4096]{1,0:T(8,128)(2,1)} %param.11) | copy-start | bytes 3145732
  39.5 12.4 %copy-start.25 = (f32[4,6]{1,0:T(4,128)S(1)}, f32[4,6]{1,0:T(4,128)}, u32[]{:S(2)}) copy-start(f32[4,6]{1,0:T(4,128)} %param.14) | copy-start | bytes 292
  39.5 12.5 %copy-start.27 = (f32[3]{0:T(128)S(1)}, f32[3]{0:T(128)}, u32[]{:S(2)}) copy-start(f32[3]{0:T(128)} %param.15) | copy-start | bytes 40
  47.2 21.5 %copy-start.7 = (f32[6,4096]{1,0:T(8,128)S(1)}, f32[6,4096]{1,0:T(8,128)}, u32[]{:S(2)}) copy-start(f32[6,4096]{1,0:T(8,128)} %param.13) | copy-start | bytes 294916
  47.2 21.5 %copy-start.18 = (f32[4096]{0:T(1024)S(1)}, f32[4096]{0:T(1024)}, u32[]{:S(2)}) copy-start(f32[4096]{0:T(1024)} %param.12) | copy-start | bytes 49156
  51.8 2.8 %copy-start.19 = (f32[128,4,6]{0,1,2:T(4,128)}, f32[128,4,6]{0,1,2:T(4,128)S(1)}, u32[]{:S(2)}) copy-start(f32[128,4,6]{0,1,2:T(4,128)S(1)} %get-tuple-element.20) | copy-start | bytes 36868
  51.8 3.3 %copy-start.20 = (f32[128,4]{0,1:T(4,128)}, f32[128,4]{0,1:T(4,128)S(1)}, u32[]{:S(2)}) copy-start(f32[128,4]{0,1:T(4,128)S(1)} %get-tuple-element.21) | copy-start | bytes 6148
  171.9 5.6 %copy-start.1 = (bf16[128,1,4096]{2,1,0:T(2,128)(2,1)S(1)}, bf16[128,1,4096]{2,1,0:T(2,128)(2,1)}, u32[]{:S(2)}) copy-start(bf16[128,1,4096]{2,1,0:T(2,128)(2,1)} %get-tuple-element.25) | copy-start | bytes 3145732
  172.0 5.6 %copy-start.3 = (bf16[128,1,4096]{2,1,0:T(2,128)(2,1)S(1)}, bf16[128,1,4096]{2,1,0:T(2,128)(2,1)}, u32[]{:S(2)}) copy-start(bf16[128,1,4096]{2,1,0:T(2,128)(2,1)} %get-tuple-element.27) | copy-start | bytes 3145732
  177.6 3.9 %copy-start.2 = (bf16[128,1,4096]{2,1,0:T(2,128)(2,1)S(1)}, bf16[128,1,4096]{2,1,0:T(2,128)(2,1)}, u32[]{:S(2)}) copy-start(bf16[128,1,4096]{2,1,0:T(2,128)(2,1)} %get-tuple-element.26) | copy-start | bytes 3145732
  177.6 3.9 %copy-start.21 = (f32[128]{0:T(128)S(1)}, f32[128]{0:T(128)}, u32[]{:S(2)}) copy-start(f32[128]{0:T(128)} %get-tuple-element.37) | copy-start | bytes 1540
  177.6 3.9 %copy-start.22 = (f32[128]{0:T(128)S(1)}, f32[128]{0:T(128)}, u32[]{:S(2)}) copy-start(f32[128]{0:T(128)} %get-tuple-element.38) | copy-start | bytes 1540
  177.6 3.9 %copy-start.23 = (f32[128]{0:T(128)S(1)}, f32[128]{0:T(128)}, u32[]{:S(2)}) copy-start(f32[128]{0:T(128)} %get-tuple-element.39) | copy-start | bytes 1540
  177.6 3.9 %copy-start.24 = (f32[128]{0:T(128)S(1)}, f32[128]{0:T(128)}, u32[]{:S(2)}) copy-start(f32[128]{0:T(128)} %get-tuple-element.40) | copy-start | bytes 1540
  181.5 9.9 %copy-start = (bf16[128,4,4096]{2,1,0:T(4,128)(2,1)S(1)}, bf16[128,4,4096]{2,1,0:T(4,128)(2,1)}, u32[]{:S(2)}) copy-start(bf16[128,4,4096]{2,1,0:T(4,128)(2,1)} %param.8) | copy-start | bytes 12582916
  181.6 9.9 %copy-start.5 = (f32[128,4096]{1,0:T(8,128)S(1)}, f32[128,4096]{1,0:T(8,128)}, u32[]{:S(2)}) copy-start(f32[128,4096]{1,0:T(8,128)} %convert_element_type.14) | copy-start | bytes 6291460
  181.6 9.9 %copy-start.9 = (f32[1,4096]{1,0:T(1,128)S(1)}, f32[1,4096]{1,0:T(1,128)}, u32[]{:S(2)}) copy-start(f32[1,4096]{1,0:T(1,128)} %copy-done.8) | copy-start | bytes 49156
  181.6 9.9 %copy-start.11 = (f32[1,4096]{1,0:T(1,128)S(1)}, f32[1,4096]{1,0:T(1,128)}, u32[]{:S(2)}) copy-start(f32[1,4096]{1,0:T(1,128)} %copy-done.10) | copy-start | bytes 49156
  181.6 9.9 %copy-start.13 = (f32[1,4096]{1,0:T(1,128)S(1)}, f32[1,4096]{1,0:T(1,128)}, u32[]{:S(2)}) copy-start(f32[1,4096]{1,0:T(1,128)} %copy-done.12) | copy-start | bytes 49156
  181.6 9.9 %copy-start.15 = (f32[1,4096]{1,0:T(1,128)S(1)}, f32[1,4096]{1,0:T(1,128)}, u32[]{:S(2)}) copy-start(f32[1,4096]{1,0:T(1,128)} %copy-done.14) | copy-start | bytes 49156
  181.6 9.9 %copy-start.17 = (f32[1,4096]{1,0:T(1,128)S(1)}, f32[1,4096]{1,0:T(1,128)}, u32[]{:S(2)}) copy-start(f32[1,4096]{1,0:T(1,128)} %copy-done.16) | copy-start | bytes 49156
Sparse Core Ops, SparseCore 0:
  70.2 107.7 all-reduce.3
where the time goes:
time: 226 us; the launch traced here: 222 us
  blocking collectives  82.6 us (37%)
  other arithmetic  77.6 us (34%)
  local copies, waits for them, and re-layouts  24.5 us (11%)
  matrix products  22.3 us (10%)
  between operations  14.9 us (7%)
    psum x1, blocking collectives, shards(): proj_sum, gain_sum = lax.psum((proj_part, gain_part), 'dp')  78.2 us
    convert_element_type x1, other arithmetic, shards(): stream_grad = total.astype(jnp.bfloat16)  20.9 us
    slice x1, local copies, waits for them, and re-layouts, shards(): cotangent[:, stream, :][:, None, :]  16.2 us
    unnamed x1, other arithmetic  15.9 us
    reduce_sum x1, other arithmetic, shards(): jnp.sum(dlin[:, :, column][..., None] * streams, axis=(0, 1))  13.4 us
    convert_element_type x1, other arithmetic, shards(): out_grad = out_total.astype(jnp.bfloat16)  9.84 us
    mul x2, other arithmetic, shards(): coef[:, :, 2 + stream][..., None] * cotangent[:, stream, :][:, None, :]  9.45 us
    dot_general x1, matrix products, shards(): jnp.einsum('tjd,tkd->tjk', streams, cotangent, preferred_element_type=jnp...  9.04 us
  transfers between devices with their start and end apart: 1, of which 0 were waited for; matrix products, arithmetic and copies ran while one was open for 29% of the time, Pallas kernels for 0%

commit v1 on v0

v1 whole, which is shorter than its diff:
```python
import jax
import jax.numpy as jnp
from jax import lax
from jax.experimental import pallas as pl
from jax.experimental.pallas import tpu as pltpu
from jax.sharding import PartitionSpec as P

F32 = jnp.float32
BF16 = jnp.bfloat16
HIGHEST = lax.Precision.HIGHEST
COLUMNS = 6
PAD = 8
QUARTERS = 4
STAT_TOKENS = 32
MIX_TOKENS = 16
VMEM_LIMIT = 30 * 1024 * 1024


def dot(a, b, dims, precision=None):
    return lax.dot_general(a, b, ((dims[0:1], dims[1:2]), ((), ())), precision=precision, preferred_element_type=F32)


def iota(shape, axis):
    return lax.broadcasted_iota(jnp.int32, shape, axis)


def split(value):
    high = value.astype(BF16)
    return high, (value - high.astype(F32)).astype(BF16)


def select_rows(shape, rows):
    row, lane = iota(shape, 0), iota(shape, 1)
    picked = jnp.zeros(shape, jnp.bool_)
    for index, first, count, step in rows:
        inside = (row == index) & (lane >= first) & (lane < first + count)
        picked = picked | (inside & ((lane - first) % step == 0))
    return picked.astype(F32)


def statistics(h_ref, g_ref, y_ref, g0_ref, gain_ref, proj_ref, stat_ref, hr_ref, gr_ref, w_ref):
    tokens, streams, width = h_ref.shape
    rows = tokens * streams

    @pl.when(pl.program_id(0) == 0)
    def _():
        high, low = split(gain_ref[...] * proj_ref[...])
        none = jnp.zeros((PAD - COLUMNS, width), F32)
        w_ref[...] = jnp.concatenate([high.astype(F32), none, low.astype(F32), none], axis=0).astype(BF16)

    own = pl.ds(pl.multiple_of(pl.program_id(0) * rows, rows), rows)
    h = h_ref[...].reshape(rows, width)
    g = g_ref[...].reshape(rows, width)
    hr_ref[own, :] = h
    gr_ref[own, :] = g
    left = jnp.concatenate([h, g], axis=0)
    right = jnp.concatenate([g, g0_ref[...], w_ref[...], y_ref[...]], axis=0)
    product = dot(left, right, (1, 1))
    at_g0, at_w, at_y, end = rows, rows + tokens, rows + tokens + 2 * PAD, rows + 2 * tokens + 2 * PAD
    token, lane = iota((rows, end), 0) // streams, iota((rows, end), 1)
    of_h = ((lane < at_g0) & (lane // streams == token)) | (lane - at_g0 == token) | ((lane >= at_w) & (lane < at_y))
    of_g = lane - at_y == token
    picked = jnp.where(of_h, product[:rows], 0.0) + jnp.where(of_g, product[rows:], 0.0)
    gather = [(0, at_y, tokens, 1), (1, at_g0, tokens, 1)]
    gather += [(2 + k, k, rows - k, streams) for k in range(streams)]
    gather += [(PAD + c, at_w + c, PAD + 1, PAD) for c in range(COLUMNS)]
    stat = dot(select_rows((2 * PAD, end), gather), picked, (1, 1), HIGHEST)
    lanes = 128
    square = jnp.zeros((rows, lanes), F32)
    for start in range(0, width, lanes):
        part = h[:, start : start + lanes].astype(F32)
        square = square + part * part
    stat_ref[...] = stat + dot(select_rows((2 * PAD, lanes), [(COLUMNS, 0, lanes, 1)]), square, (1, 1), HIGHEST)


def scales_of(scale_ref, shape):
    row = iota(shape, 0)
    return jnp.where(row == 0, scale_ref[0], jnp.where(row == 1, scale_ref[1], scale_ref[2]))


def partials(full_width, *refs):
    *stat_refs, scale_ref, hr_ref, coef_ref, dw_ref = refs
    total = stat_refs[0][...]
    for ref in stat_refs[1:]:
        total = total + ref[...]
    dcoef, lin = total[:PAD], total[PAD:]
    square = dcoef[COLUMNS : COLUMNS + 1]
    inv_rms = lax.rsqrt(square / full_width + 1e-06)
    bent = jnp.tanh(inv_rms * lin)
    scales = scales_of(scale_ref, bent.shape)
    dpre = jnp.where(iota(bent.shape, 0) < COLUMNS, dcoef * scales * (1.0 - bent * bent), 0.0)
    dlin = dpre * inv_rms
    dsquare = -0.5 * inv_rms * inv_rms * inv_rms / full_width * jnp.sum(dpre * lin, axis=0, keepdims=True)
    high, low = split(dlin)
    left = jnp.concatenate([high.astype(F32), low.astype(F32)], axis=0).astype(BF16)
    coef_ref[0:PAD] = scales * bent
    coef_ref[PAD : 2 * PAD] = dlin
    coef_ref[2 * PAD : 3 * PAD] = jnp.broadcast_to(2.0 * dsquare, bent.shape)
    both = dot(left, hr_ref[...], (1, 0))
    dw = both[:PAD] + both[PAD:]
    part = dw.shape[1] // QUARTERS
    for q in range(QUARTERS):
        dw_ref[q * COLUMNS : (q + 1) * COLUMNS, :] = dw[:COLUMNS, q * part : (q + 1) * part]


def outputs(coef_ref, mix_ref, hr_ref, gr_ref, g0_ref, w_ref, *refs):
    grad_ref, out_ref = refs[-2:]
    tokens, streams, width = grad_ref.shape
    coef = coef_ref[...]
    bent = coef[:PAD]
    row, stream = iota(bent.shape, 0), iota(bent.shape, 1) % streams
    static = jnp.zeros(bent.shape, F32)
    for j in range(streams):
        for c in range(COLUMNS):
            static = jnp.where((row == c) & (stream == j), mix_ref[j, c], static)
    coef = jnp.concatenate([static + bent, coef[PAD:]], axis=0)
    group = min(MIX_TOKENS, tokens)
    rows = group * streams
    at_g0, at_w, at_h, end = rows, rows + group, rows + group + 2 * PAD, 2 * rows + group + 2 * PAD
    spread = [(1, at_g0, group, 1), (2 * PAD, at_h, rows, 1)]
    spread += [(2 + k, k, rows - k, streams) for k in range(streams)]
    spread += [(PAD + c, at_w + c, PAD + 1, PAD) for c in range(COLUMNS)]
    spread = select_rows((3 * PAD, end), spread)
    token, line, lane = iota((rows, end), 0) // streams, iota((rows, end), 0), iota((rows, end), 1)
    kept = ((lane < at_g0) & (lane // streams == token)) | (lane - at_g0 == token) | (lane - at_h == line)
    kept = kept | ((lane >= at_w) & (lane < at_h))
    out_token, out_lane = iota((group, end), 0), iota((group, end), 1)
    out_kept = (out_lane < at_g0) & (out_lane // streams == out_token)
    step = min(width, 1024)
    for start in range(0, tokens, group):
        here = coef[:, start * streams : start * streams + rows]
        high, low = split(jnp.where(kept, dot(here, spread, (0, 0), HIGHEST), 0.0))
        beta = jnp.concatenate([here[0:1], jnp.zeros((1, end - rows), F32)], axis=1)
        out_high, out_low = split(jnp.where(out_kept, jnp.broadcast_to(beta, (group, end)), 0.0))
        left = jnp.concatenate([high, low, out_high, out_low], axis=0)
        own = pl.ds(start * streams, rows)
        for column in range(0, width, step):
            at = pl.ds(column, step)
            right = jnp.concatenate(
                [gr_ref[own, at], g0_ref[start : start + group, at], w_ref[:, at], hr_ref[own, at]], axis=0
            )
            result = dot(left, right, (1, 0))
            total = result[:rows] + result[rows : 2 * rows]
            grad_ref[start : start + group, :, at] = total.astype(BF16).reshape(group, streams, step)
            out_ref[start : start + group, at] = (
                result[2 * rows : 2 * rows + group] + result[2 * rows + group :]
            ).astype(BF16)


def whole(*shape):
    return pl.BlockSpec(shape, lambda *_: (0,) * len(shape))


def shards(streams, layer_out, cotangent, input_cot, gain, projection, static_mix, tanh_scale):
    tokens, count, width = streams.shape
    rows = tokens * count
    dp, tensor = lax.axis_size("dp"), lax.axis_size("tensor")
    full_width = width * tensor
    params = pltpu.CompilerParams(vmem_limit_bytes=VMEM_LIMIT)
    scalars = pl.BlockSpec(memory_space=pltpu.SMEM)

    block = min(STAT_TOKENS, tokens)
    def in_hbm(array):
        return pltpu.with_memory_space_constraint(array, pltpu.HBM)

    streams, cotangent, layer_out, input_cot = map(in_hbm, (streams, cotangent, layer_out, input_cot))
    wide = pl.BlockSpec((block, count, width), lambda i: (i, 0, 0))
    flat = pl.BlockSpec((block, width), lambda i: (i, 0))
    stat, hr, gr, w = pl.pallas_call(
        statistics,
        grid=(tokens // block,),
        in_specs=[wide, wide, flat, flat, whole(1, width), whole(COLUMNS, width)],
        out_specs=[
            pl.BlockSpec((2 * PAD, block * count), lambda i: (0, i)),
            whole(rows, width),
            whole(rows, width),
            whole(2 * PAD, width),
        ],
        out_shape=[
            jax.ShapeDtypeStruct((2 * PAD, rows), F32),
            jax.ShapeDtypeStruct((rows, width), BF16),
            jax.ShapeDtypeStruct((rows, width), BF16),
            jax.ShapeDtypeStruct((2 * PAD, width), BF16),
        ],
        compiler_params=params,
        name="statistics",
    )(streams, cotangent, layer_out, input_cot, in_hbm(gain.reshape(1, width)), in_hbm(projection))

    if tensor == 2:
        stats = (stat, lax.ppermute(stat, "tensor", [(0, 1), (1, 0)]))
    else:
        stats = (lax.psum(stat, "tensor"),)

    coef, dw = pl.pallas_call(
        lambda *refs: partials(float(full_width), *refs),
        in_specs=[pl.BlockSpec(memory_space=pltpu.VMEM)] * len(stats) + [scalars, pl.BlockSpec(memory_space=pltpu.VMEM)],
        out_specs=[pl.BlockSpec(memory_space=pltpu.VMEM)] * 2,
        out_shape=[
            jax.ShapeDtypeStruct((3 * PAD, rows), F32),
            jax.ShapeDtypeStruct((QUARTERS * COLUMNS, width // QUARTERS), F32),
        ],
        compiler_params=params,
        name="partials",
    )(*stats, tanh_scale, hr)

    def mixed(index, previous):
        wide_at = pl.BlockSpec((block, count, width), lambda i: (index, 0, 0))
        flat_at = pl.BlockSpec((block, width), lambda i: (index, 0))
        lines = pl.BlockSpec((block * count, width), lambda i: (index, 0))
        return pl.pallas_call(
            outputs,
            grid=(1,),
            in_specs=[
                pl.BlockSpec((3 * PAD, block * count), lambda i: (0, index)),
                scalars,
                lines,
                lines,
                flat_at,
                whole(2 * PAD, width),
            ]
            + [pl.BlockSpec(memory_space=pl.ANY)] * len(previous),
            out_specs=[wide_at, flat_at],
            out_shape=[
                jax.ShapeDtypeStruct((tokens, count, width), BF16),
                jax.ShapeDtypeStruct((tokens, width), BF16),
            ],
            input_output_aliases={6 + i: i for i in range(len(previous))},
            compiler_params=params,
            cost_estimate=pl.CostEstimate(flops=4_000_000_000, bytes_accessed=block * width * 30, transcendentals=0),
            name="outputs",
        )(coef, static_mix, hr, gr, input_cot, w, *previous)

    grads = ()
    for index in range(tokens // block):
        grads = mixed(index, grads)
    stream_grad, out_grad = grads

    if dp & (dp - 1) == 0:
        step = 1
        while step < dp:
            dw = dw + lax.ppermute(dw, "dp", [(i, i ^ step) for i in range(dp)])
            step *= 2
    else:
        dw = lax.psum(dw, "dp")
    part = width // QUARTERS
    dw = jnp.concatenate([dw[q * COLUMNS : (q + 1) * COLUMNS] for q in range(QUARTERS)], axis=1)
    all_tokens = tokens * dp
    proj_grad = gain[None, :] * dw / jnp.sqrt(float(count) * all_tokens * full_width)
    gain_grad = jnp.sum(dw * projection, axis=0) / jnp.sqrt(float(count) * all_tokens)
    return (stream_grad, out_grad, proj_grad, gain_grad)


def solution(mesh):
    placed = (
        P("dp", None, "tensor"),
        P("dp", "tensor"),
        P("dp", None, "tensor"),
        P("dp", "tensor"),
        P("tensor"),
        P(None, "tensor"),
        P(),
        P(),
    )
    return jax.shard_map(
        shards,
        mesh=mesh,
        in_specs=placed,
        out_specs=(P("dp", None, "tensor"), P("dp", "tensor"), P(None, "tensor"), P("tensor")),
        check_vma=False,
    )
```

time: 226 us -> 36.7 us (0.16); the launches traced: 222 us -> 36.4 us
  blocking collectives: 82.6 us -> 0 us
  other arithmetic: 77.6 us -> 1.36 us
  local copies, waits for them, and re-layouts: 24.5 us -> 0.03 us
  Pallas kernels: 0 us -> 23.4 us
  matrix products: 22.3 us -> 0 us
  between operations: 14.9 us -> 0.71 us
  starting transfers between devices: 0.04 us -> 9.27 us
    psum x2 -> x0, blocking collectives: 82.6 us -> none  [the longest x1 78.2 us: shards(): proj_sum, gain_sum = lax.psum((proj_part, gain_part), 'dp')]
    convert_element_type x3 -> x0, other arithmetic: 32.3 us -> none  [the longest x1 20.9 us: shards(): stream_grad = total.astype(jnp.bfloat16)]
    pallas_call x0 -> x6, Pallas kernels: none -> 23.4 us  [the longest x4 14 us: mixed(): pl.pallas_call(outputs, grid=(1,), in_specs=[pl.BlockSpec((3 * PAD, block...]
    dot_general x3 -> x0, matrix products: 22.3 us -> none  [the longest x1 9.04 us: shards(): jnp.einsum('tjd,tkd->tjk', streams, cotangent, preferred_element_type=jnp...]
    slice x3 -> x1, local copies, waits for them, and re-layouts: 16.8 us -> 0.01 us  [shards(): dw[q * COLUMNS:(q + 1) * COLUMNS]]
    unnamed x1 -> x0, other arithmetic: 15.9 us -> none
    reduce_sum x3 -> x1, other arithmetic: 15.4 us -> 0.7 us  [shards(): jnp.sum(dw * projection, axis=0) / jnp.sqrt(float(count) * all_tokens)]
    mul x5 -> x0, other arithmetic: 11.7 us -> none  [the longest x2 9.45 us: shards(): coef[:, :, 2 + stream][..., None] * cotangent[:, stream, :][:, None, :]]
  transfers between devices with their start and end apart: 1 -> 5, of which waited for: 0 -> 2; matrix products, arithmetic and copies ran while one was open for 29% -> 0% of each run, Pallas kernels for 0% -> 39%
where the time goes in v1:
time: 36.7 us; the launch traced here: 36.4 us
  Pallas kernels  23.4 us (64%)
  starting transfers between devices  9.27 us (25%)
  waiting for transfers between devices  1.63 us (4%)
  other arithmetic  1.36 us (4%)
  between operations  0.71 us (2%)
    pallas_call x4, Pallas kernels, mixed(): pl.pallas_call(outputs, grid=(1,), in_specs=[pl.BlockSpec((3 * PAD, block...  14 us
    ppermute x4, starting transfers between devices, shards(): dw = dw + lax.ppermute(dw, 'dp', [(i, i ^ step) for i in range(dp)])  8.71 us
    pallas_call x1, Pallas kernels, shards(): pl.pallas_call(statistics, grid=(tokens // block,), in_specs=[wide, wide,...  8.18 us
    pallas_call x1, Pallas kernels, shards(): pl.pallas_call(lambda *refs: partials(float(full_width), *refs), in_specs...  1.19 us
    ppermute x1, waiting for transfers between devices, shards(): stats = (stat, lax.ppermute(stat, 'tensor', [(0, 1), (1, 0)]))  0.86 us
    ppermute x4, waiting for transfers between devices, shards(): dw = dw + lax.ppermute(dw, 'dp', [(i, i ^ step) for i in range(dp)])  0.77 us
  transfers between devices with their start and end apart: 5, of which 2 were waited for; matrix products, arithmetic and copies ran while one was open for 0% of the time, Pallas kernels for 39%

profile of v1, /device:TPU:0, one launch (start us, length us, event | category | flops | bytes accessed | tf_op | source)
XLA Modules:
  0.0 36.4 jit_solution(1515924247639965408)
XLA Ops:
  0.6 0.0 copy-start.1
  0.6 8.2 %statistics.1 = (f32[16,512]{1,0:T(8,128)S(1)}, bf16[512,4096]{1,0:T(8,128)(2,1)S(1)}, bf16[512,4096]{1,0:T(8,128)(2,1)S(1)}, bf16[16,4096]{1,0:T(8,128)(2,1)S(1)}) custom-call(bf16[128,4,4096]{2,1,0:T(4,128)(2,1)} %h_ref.1, bf16[128,4,4096]{2,1,0:T(4,128)(2,1)} %g_ref.1, bf16[128,4096]{1,0:T(8,128)(2,1)} %y_ref.1, bf16[128,4096]{1,0:T(8,128)(2,1)} %g0_ref.9, ...), custom_call_target="tpu_custom_call" | custom-call | tf_op jit(solution)/shard_map/statistics/pallas_call | solution.py:169
  8.8 0.0 copy-start
  8.9 0.6 %collective-permute-start = (f32[16,512]{1,0:T(8,128)S(1)}, f32[16,512]{1,0:T(8,128)S(1)}, u32[]{:S(2)}, u32[]{:S(2)}) collective-permute-start(f32[16,512]{1,0:T(8,128)S(1)} %get-tuple-element.18.refs_0_), channel_id=1, source_target_pairs={{0,1},{1,0},{2,3},{3,2},{4,5},{5,4},{6,7},{7,6},{8,9},{9,8},{10,11... | collective-permute-start | bytes 98312 | tf_op jit(solution)/shard_map/ppermute | solution.py:190
  9.4 0.9 %collective-permute-done.refs_1_ = f32[16,512]{1,0:T(8,128)S(1)} collective-permute-done((f32[16,512]{1,0:T(8,128)S(1)}, f32[16,512]{1,0:T(8,128)S(1)}, u32[]{:S(2)}, u32[]{:S(2)}) %collective-permute-start) | collective-permute-done | bytes 32800 | tf_op jit(solution)/shard_map/ppermute | solution.py:190
  10.3 0.0 copy-done.1
  10.3 1.2 %partials.1 = (f32[24,512]{1,0:T(8,128)S(1)}, f32[24,1024]{1,0:T(8,128)S(1)}) custom-call(f32[16,512]{1,0:T(8,128)S(1)} %get-tuple-element.18.refs_0_, f32[16,512]{1,0:T(8,128)S(1)} %collective-permute-done.refs_1_, f32[3]{0:T(128)S(1)} %copy-done.1, bf16[512,4096]{1,0:T(8,128)(2,1)S(1)} %get-tuple-element.19.refs_3_.hr_ref), custom_call_target="tpu_custom_call" | custom-call | tf_op jit(solution)/shard_map/partials/pallas_call | solution.py:194
  11.5 2.8 %collective-permute-start.1 = (f32[24,1024]{1,0:T(8,128)S(1)}, f32[24,1024]{1,0:T(8,128)S(1)}, u32[]{:S(2)}, u32[]{:S(2)}) collective-permute-start(f32[24,1024]{1,0:T(8,128)S(1)} %get-tuple-element.31), channel_id=1, source_target_pairs={{0,2},{2,0},{4,6},{6,4},{8,10},{10,8},{12,14},{14,12},{16,18},{18,... | collective-permute-start | bytes 294920 | tf_op jit(solution)/shard_map/ppermute | solution.py:241
  14.3 0.0 copy-done
  14.3 3.5 %outputs.4 = (bf16[128,4,4096]{2,1,0:T(4,128)(2,1)}, bf16[128,4096]{1,0:T(8,128)(2,1)}) custom-call(f32[24,512]{1,0:T(8,128)S(1)} %get-tuple-element.20.coef_ref, f32[4,6]{1,0:T(4,128)S(1)} %copy-done, bf16[512,4096]{1,0:T(8,128)(2,1)S(1)} %get-tuple-element.19.refs_3_.hr_ref, bf16[512,4096]{1,0:T(8,128)(2,1)S(1)} %get-tuple-element.21.gr_ref, ...), custom_call_target="tpu_custom_call" | custom-call | flops 4000000000 | bytes 3932160 | tf_op jit(solution)/shard_map/outputs/pallas_call | solution.py:210
  17.8 0.0 collective-permute-done.1
  17.8 1.6 %collective-permute-start.2 = (f32[24,1024]{1,0:T(8,128)S(1)}, f32[24,1024]{1,0:T(8,128)S(1)}, u32[]{:S(2)}, u32[]{:S(2)}) collective-permute-start(f32[24,1024]{1,0:T(8,128)S(1)} %add.12), channel_id=1, source_target_pairs={{0,4},{2,6},{4,0},{6,2},{8,12},{10,14},{12,8},{14,10},{16,20},{18,... | collective-permute-start | bytes 294920 | tf_op jit(solution)/shard_map/ppermute | solution.py:241
  19.4 3.5 %outputs.5 = (bf16[128,4,4096]{2,1,0:T(4,128)(2,1)}, bf16[128,4096]{1,0:T(8,128)(2,1)}) custom-call(f32[24,512]{1,0:T(8,128)S(1)} %get-tuple-element.20.coef_ref, f32[4,6]{1,0:T(4,128)S(1)} %copy-done, bf16[512,4096]{1,0:T(8,128)(2,1)S(1)} %get-tuple-element.19.refs_3_.hr_ref, ...), custom_call_target="tpu_custom_call", output_to_operand_aliasing={{0}: (6, {}), {1}: (7, {})} | custom-call | flops 4000000000 | bytes 3932160 | tf_op jit(solution)/shard_map/outputs/pallas_call | solution.py:210
  22.9 0.0 collective-permute-done.2
  23.0 1.6 %collective-permute-start.3 = (f32[24,1024]{1,0:T(8,128)S(1)}, f32[24,1024]{1,0:T(8,128)S(1)}, u32[]{:S(2)}, u32[]{:S(2)}) collective-permute-start(f32[24,1024]{1,0:T(8,128)S(1)} %add.13), channel_id=1, source_target_pairs={{0,8},{2,10},{4,12},{6,14},{8,0},{10,2},{12,4},{14,6},{16,24},{18,... | collective-permute-start | bytes 294920 | tf_op jit(solution)/shard_map/ppermute | solution.py:241
  24.6 3.5 %outputs.6 = (bf16[128,4,4096]{2,1,0:T(4,128)(2,1)}, bf16[128,4096]{1,0:T(8,128)(2,1)}) custom-call(f32[24,512]{1,0:T(8,128)S(1)} %get-tuple-element.20.coef_ref, f32[4,6]{1,0:T(4,128)S(1)} %copy-done, bf16[512,4096]{1,0:T(8,128)(2,1)S(1)} %get-tuple-element.19.refs_3_.hr_ref, ...), custom_call_target="tpu_custom_call", output_to_operand_aliasing={{0}: (6, {}), {1}: (7, {})} | custom-call | flops 4000000000 | bytes 3932160 | tf_op jit(solution)/shard_map/outputs/pallas_call | solution.py:210
  28.1 0.0 collective-permute-done.3
  28.1 2.7 %collective-permute-start.4 = (f32[24,1024]{1,0:T(8,128)S(1)}, f32[24,1024]{1,0:T(8,128)S(1)}, u32[]{:S(2)}, u32[]{:S(2)}) collective-permute-start(f32[24,1024]{1,0:T(8,128)S(1)} %add.14), channel_id=1, source_target_pairs={{0,16},{2,18},{4,20},{6,22},{8,24},{10,26},{12,28},{14,30},{16,0},... | collective-permute-start | bytes 294920 | tf_op jit(solution)/shard_map/ppermute | solution.py:241
  30.8 0.0 copy-start.2
  30.8 0.0 copy-start.3
  30.8 3.5 %outputs.7 = (bf16[128,4,4096]{2,1,0:T(4,128)(2,1)}, bf16[128,4096]{1,0:T(8,128)(2,1)}) custom-call(f32[24,512]{1,0:T(8,128)S(1)} %get-tuple-element.20.coef_ref, f32[4,6]{1,0:T(4,128)S(1)} %copy-done, bf16[512,4096]{1,0:T(8,128)(2,1)S(1)} %get-tuple-element.19.refs_3_.hr_ref, ...), custom_call_target="tpu_custom_call", output_to_operand_aliasing={{0}: (6, {}), {1}: (7, {})} | custom-call | flops 4000000000 | bytes 3932160 | tf_op jit(solution)/shard_map/outputs/pallas_call | solution.py:210
  34.3 0.8 %collective-permute-done.4 = f32[24,1024]{1,0:T(8,128)S(1)} collective-permute-done((f32[24,1024]{1,0:T(8,128)S(1)}, f32[24,1024]{1,0:T(8,128)S(1)}, u32[]{:S(2)}, u32[]{:S(2)}) %collective-permute-start.4) | collective-permute-done | bytes 98336 | tf_op jit(solution)/shard_map/ppermute | solution.py:241
  35.1 0.0 copy-done.2
  35.1 0.0 copy-done.3
  35.1 0.7 %multiply_reduce_fusion = (f32[4096]{0:T(1024)S(1)}, f32[6,4096]{1,0:T(8,128)}) fusion(f32[6,4096]{1,0:T(8,128)S(1)} %copy-done.2, f32[6,1024]{1,0:T(8,128)S(1)} %get-tuple-element.35, f32[6,1024]{1,0:T(8,128)S(1)} %get-tuple-element.36, f32[6,1024]{1,0:T(8,128)S(1)} %get-tuple-element.37, f32[6,1024]{1,0:T(8,128)S(1)} %get-tuple-element.34, ...), kind=kLoop, calls=%fused_computation.1 | loop fusion | flops 167936 | bytes 327680 | tf_op jit(solution)/shard_map/reduce_sum | solution.py:249
  35.8 0.6 %broadcast_multiply_fusion = f32[4096]{0:T(1024)} fusion(f32[4096]{0:T(1024)S(1)} %get-tuple-element.32), kind=kLoop, calls=%fused_computation.3 | loop fusion | flops 4096 | bytes 32768 | tf_op jit(solution)/shard_map/div | solution.py:249
  (5 shorter events, 0.1 us)
Async XLA Ops:
  0.6 9.7 %copy-start.1 = (f32[3]{0:T(128)S(1)}, f32[3]{0:T(128)}, u32[]{:S(2)}) copy-start(f32[3]{0:T(128)} %refs_2_.1) | copy-start | bytes 40
  8.8 5.5 %copy-start = (f32[4,6]{1,0:T(4,128)S(1)}, f32[4,6]{1,0:T(4,128)}, u32[]{:S(2)}) copy-start(f32[4,6]{1,0:T(4,128)} %mix_ref.7) | copy-start | bytes 292
  8.9 1.4 %collective-permute-start = (f32[16,512]{1,0:T(8,128)S(1)}, f32[16,512]{1,0:T(8,128)S(1)}, u32[]{:S(2)}, u32[]{:S(2)}) collective-permute-start(f32[16,512]{1,0:T(8,128)S(1)} %get-tuple-element.18.refs_0_), channel_id=1, source_target_pairs={{0,1},{1,0},{2,3},{3,2},{4,5},{5,4},{6,7},{7,6},{8,9},{9,8},{10,11... | collective-permute-start | bytes 98312 | tf_op jit(solution)/shard_map/ppermute | solution.py:190
  11.5 6.3 %collective-permute-start.1 = (f32[24,1024]{1,0:T(8,128)S(1)}, f32[24,1024]{1,0:T(8,128)S(1)}, u32[]{:S(2)}, u32[]{:S(2)}) collective-permute-start(f32[24,1024]{1,0:T(8,128)S(1)} %get-tuple-element.31), channel_id=1, source_target_pairs={{0,2},{2,0},{4,6},{6,4},{8,10},{10,8},{12,14},{14,12},{16,18},{18,... | collective-permute-start | bytes 294920 | tf_op jit(solution)/shard_map/ppermute | solution.py:241
  17.8 5.1 %collective-permute-start.2 = (f32[24,1024]{1,0:T(8,128)S(1)}, f32[24,1024]{1,0:T(8,128)S(1)}, u32[]{:S(2)}, u32[]{:S(2)}) collective-permute-start(f32[24,1024]{1,0:T(8,128)S(1)} %add.12), channel_id=1, source_target_pairs={{0,4},{2,6},{4,0},{6,2},{8,12},{10,14},{12,8},{14,10},{16,20},{18,... | collective-permute-start | bytes 294920 | tf_op jit(solution)/shard_map/ppermute | solution.py:241
  23.0 5.1 %collective-permute-start.3 = (f32[24,1024]{1,0:T(8,128)S(1)}, f32[24,1024]{1,0:T(8,128)S(1)}, u32[]{:S(2)}, u32[]{:S(2)}) collective-permute-start(f32[24,1024]{1,0:T(8,128)S(1)} %add.13), channel_id=1, source_target_pairs={{0,8},{2,10},{4,12},{6,14},{8,0},{10,2},{12,4},{14,6},{16,24},{18,... | collective-permute-start | bytes 294920 | tf_op jit(solution)/shard_map/ppermute | solution.py:241
  28.1 7.0 %collective-permute-start.4 = (f32[24,1024]{1,0:T(8,128)S(1)}, f32[24,1024]{1,0:T(8,128)S(1)}, u32[]{:S(2)}, u32[]{:S(2)}) collective-permute-start(f32[24,1024]{1,0:T(8,128)S(1)} %add.14), channel_id=1, source_target_pairs={{0,16},{2,18},{4,20},{6,22},{8,24},{10,26},{12,28},{14,30},{16,0},... | collective-permute-start | bytes 294920 | tf_op jit(solution)/shard_map/ppermute | solution.py:241
  30.8 4.3 %copy-start.2 = (f32[6,4096]{1,0:T(8,128)S(1)}, f32[6,4096]{1,0:T(8,128)}, u32[]{:S(2)}) copy-start(f32[6,4096]{1,0:T(8,128)} %proj_ref.1) | copy-start | bytes 294916
  30.8 4.4 %copy-start.3 = (f32[4096]{0:T(1024)S(1)}, f32[4096]{0:T(1024)}, u32[]{:S(2)}) copy-start(f32[4096]{0:T(1024)} %param.12) | copy-start | bytes 49156

commit v2 on v1

v2 whole, which is shorter than its diff:
```python
import jax
import jax.numpy as jnp
from jax import lax
from jax.experimental import pallas as pl
from jax.experimental.pallas import tpu as pltpu
from jax.sharding import PartitionSpec as P

F32 = jnp.float32
BF16 = jnp.bfloat16
HIGHEST = lax.Precision.HIGHEST
COLUMNS = 6
PAD = 8
QUARTERS = 4
STAT_TOKENS = 32
MIX_TOKENS = 16
WINDOWS = 4
AHEAD = 2
VMEM_LIMIT = 30 * 1024 * 1024


def dot(a, b, dims, precision=None):
    return lax.dot_general(a, b, ((dims[0:1], dims[1:2]), ((), ())), precision=precision, preferred_element_type=F32)


def iota(shape, axis):
    return lax.broadcasted_iota(jnp.int32, shape, axis)


def split(value):
    high = value.astype(BF16)
    return high, (value - high.astype(F32)).astype(BF16)


def select_rows(shape, rows):
    row, lane = iota(shape, 0), iota(shape, 1)
    picked = jnp.zeros(shape, jnp.bool_)
    for index, first, count, step in rows:
        inside = (row == index) & (lane >= first) & (lane < first + count)
        picked = picked | (inside & ((lane - first) % step == 0))
    return picked.astype(F32)


def statistics(
    h_hbm, g_hbm, y_hbm, g0_hbm, gain_hbm, proj_hbm, stat_ref, hr_ref, gr_ref, g0_ref, w_ref, h_buf, g_buf, y_buf, gain_buf, proj_buf, sems, more_sems
):
    total, streams, width = h_hbm.shape
    blocks = sems.shape[0]
    tokens = total // blocks
    weights = [
        pltpu.make_async_copy(gain_hbm, gain_buf, more_sems.at[0]),
        pltpu.make_async_copy(proj_hbm, proj_buf, more_sems.at[1]),
    ]

    def copies(block):
        at = pl.ds(pl.multiple_of(block * tokens, tokens), tokens)
        pairs = [(h_hbm, h_buf), (g_hbm, g_buf), (g0_hbm, g0_ref), (y_hbm, y_buf)]
        return [
            pltpu.make_async_copy(source.at[at], target.at[at], sems.at[block, index])
            for index, (source, target) in enumerate(pairs)
        ]

    for copy in weights:
        copy.start()
    for block in range(min(AHEAD, blocks)):
        for copy in copies(block):
            copy.start(priority=block % 2)
    for copy in weights:
        copy.wait()
    high, low = split(gain_buf[...] * proj_buf[...])
    none = jnp.zeros((PAD - COLUMNS, width), F32)
    w_ref[...] = jnp.concatenate([high.astype(F32), none, low.astype(F32), none], axis=0).astype(BF16)

    @pl.loop(0, blocks)
    def _(block):
        for copy in copies(block):
            copy.wait()

        @pl.when(block + AHEAD < blocks)
        def _():
            for copy in copies(block + AHEAD):
                copy.start(priority=1)

        statistics_of(block, tokens, stat_ref, hr_ref, gr_ref, g0_ref, w_ref, h_buf, g_buf, y_buf)


def statistics_of(block, tokens, stat_ref, hr_ref, gr_ref, g0_ref, w_ref, h_buf, g_buf, y_buf):
    _, streams, width = h_buf.shape
    rows = tokens * streams
    at = pl.ds(pl.multiple_of(block * tokens, tokens), tokens)
    own = pl.ds(pl.multiple_of(block * rows, rows), rows)
    hr_ref[own, :] = h_buf[at].reshape(rows, width)
    gr_ref[own, :] = g_buf[at].reshape(rows, width)
    h = hr_ref[own, :]
    left = jnp.concatenate([gr_ref[own, :], g0_ref[at, :], w_ref[...]], axis=0)
    product = dot(left, jnp.concatenate([h, y_buf[at, :]], axis=0), (1, 1))
    lanes = 128
    square = jnp.zeros((rows, lanes), F32)
    for start in range(0, width, lanes):
        part = h[:, start : start + lanes].astype(F32)
        square = square + part * part
    square = jnp.sum(square.T, axis=0, keepdims=True)
    line, token = iota((rows, rows), 0), iota((rows, rows), 1) // streams
    mixer = jnp.where(line // streams == token, product[:rows, :rows], 0.0)
    mixer = jnp.sum(mixer.reshape(rows // PAD, PAD, rows), axis=0)
    folded = mixer[:streams]
    for start in range(streams, PAD, streams):
        folded = folded + mixer[start : start + streams]
    alpha = jnp.where(line[:tokens] == token[:tokens], product[rows : rows + tokens, :rows], 0.0)
    alpha = jnp.sum(alpha, axis=0, keepdims=True)
    beta = jnp.where(line[:tokens] == token[:tokens], product[:rows, rows:].T, 0.0)
    beta = jnp.sum(beta, axis=0, keepdims=True)
    lin = product[rows + tokens : rows + tokens + PAD, :rows] + product[rows + tokens + PAD :, :rows]
    stat_ref[:, own] = jnp.concatenate([beta, alpha, folded, square, jnp.zeros_like(square), lin], axis=0)


def scales_of(scale_ref, shape):
    row = iota(shape, 0)
    return jnp.where(row == 0, scale_ref[0], jnp.where(row == 1, scale_ref[1], scale_ref[2]))


def partials(full_width, *refs):
    *stat_refs, scale_ref, hr_ref, coef_ref, dw_ref = refs
    total = stat_refs[0][...]
    for ref in stat_refs[1:]:
        total = total + ref[...]
    dcoef, lin = total[:PAD], total[PAD:]
    square = dcoef[COLUMNS : COLUMNS + 1]
    inv_rms = lax.rsqrt(square / full_width + 1e-06)
    bent = jnp.tanh(inv_rms * lin)
    scales = scales_of(scale_ref, bent.shape)
    dpre = jnp.where(iota(bent.shape, 0) < COLUMNS, dcoef * scales * (1.0 - bent * bent), 0.0)
    dlin = dpre * inv_rms
    dsquare = -0.5 * inv_rms * inv_rms * inv_rms / full_width * jnp.sum(dpre * lin, axis=0, keepdims=True)
    high, low = split(dlin)
    left = jnp.concatenate([high.astype(F32), low.astype(F32)], axis=0).astype(BF16)
    coef = jnp.concatenate([scales * bent, dlin, jnp.broadcast_to(2.0 * dsquare, bent.shape)], axis=0)
    groups, _, lanes = coef_ref.shape
    for index in range(groups):
        coef_ref[index] = coef[:, index * lanes : (index + 1) * lanes]
    both = dot(left, hr_ref[...], (1, 0))
    dw = both[:PAD] + both[PAD:]
    part = dw.shape[1] // QUARTERS
    for q in range(QUARTERS):
        dw_ref[q * COLUMNS : (q + 1) * COLUMNS, :] = dw[:COLUMNS, q * part : (q + 1) * part]


def put(refs, first, sems):
    grad_buf, out_buf, grad_hbm, out_hbm = refs
    at = pl.ds(first, out_buf.shape[0])
    return [
        pltpu.make_async_copy(grad_buf, grad_hbm.at[at], sems.at[0]),
        pltpu.make_async_copy(out_buf, out_hbm.at[at], sems.at[1]),
    ]


def outputs(first, groups, finished, last, coef_ref, mix_ref, hr_ref, gr_ref, g0_ref, w_ref, *refs):
    *results, grad_buf, out_buf, sems, more_sems = refs
    group, streams, width = grad_buf.shape[0] // groups, grad_buf.shape[1], grad_buf.shape[2]
    copies = put((*refs[:2], *results[-2:]), first * group - refs[1].shape[0], sems) if finished else []
    for copy in copies:
        copy.start()
    rows = group * streams
    at_g0, at_w, at_h, end = rows, rows + group, rows + group + 2 * PAD, 2 * rows + group + 2 * PAD
    spread = [(1, at_g0, group, 1), (2 * PAD, at_h, rows, 1)]
    spread += [(2 + k, k, rows - k, streams) for k in range(streams)]
    spread += [(PAD + c, at_w + c, PAD + 1, PAD) for c in range(COLUMNS)]
    spread = select_rows((3 * PAD, end), spread)
    token, line, lane = iota((rows, end), 0) // streams, iota((rows, end), 0), iota((rows, end), 1)
    kept = ((lane < at_g0) & (lane // streams == token)) | (lane - at_g0 == token) | (lane - at_h == line)
    kept = kept | ((lane >= at_w) & (lane < at_h))
    out_token, out_lane = iota((group, end), 0), iota((group, end), 1)
    out_kept = (out_lane < at_g0) & (out_lane // streams == out_token)
    row, stream = iota((PAD, rows), 0), iota((PAD, rows), 1) % streams
    static = jnp.zeros((PAD, rows), F32)
    for j in range(streams):
        for c in range(COLUMNS):
            static = jnp.where((row == c) & (stream == j), mix_ref[j, c], static)
    lefts = []
    for index in range(groups):
        here = coef_ref[first + index]
        here = jnp.concatenate([static + here[:PAD], here[PAD:]], axis=0)
        high, low = split(jnp.where(kept, dot(here, spread, (0, 0), HIGHEST), 0.0))
        beta = jnp.concatenate([here[0:1], jnp.zeros((1, end - rows), F32)], axis=1)
        out_high, out_low = split(jnp.where(out_kept, jnp.broadcast_to(beta, (group, end)), 0.0))
        lefts.append(jnp.concatenate([high, low, out_high, out_low], axis=0))
    step = min(width, 1024)
    for index, left in enumerate(lefts):
        own = pl.ds((first + index) * rows, rows)
        source = pl.ds((first + index) * group, group)
        target = pl.ds(index * group, group)
        for column in range(0, width, step):
            at = pl.ds(column, step)
            right = jnp.concatenate([gr_ref[own, at], g0_ref[source, at], w_ref[:, at], hr_ref[own, at]], axis=0)
            result = dot(left, right, (1, 0))
            total = result[:rows] + result[rows : 2 * rows]
            grad_buf[target, :, at] = total.astype(BF16).reshape(group, streams, step)
            out_buf[target, at] = (result[2 * rows : 2 * rows + group] + result[2 * rows + group :]).astype(BF16)
    if last:
        own = put((grad_buf, out_buf, *results[-2:]), first * group, more_sems)
        for copy in own:
            copy.start()
        copies += own
    for copy in copies:
        copy.wait()


def tail(proj_scale, gain_scale, dw_ref, more_ref, gain_ref, proj_ref, proj_grad_ref, gain_grad_ref):
    dw = dw_ref[...] + more_ref[...]
    part = dw.shape[1]
    for q in range(QUARTERS):
        at = pl.ds(q * part, part)
        own = dw[q * COLUMNS : (q + 1) * COLUMNS]
        proj_grad_ref[:, at] = gain_ref[:, at] * own * proj_scale
        gain_grad_ref[:, at] = jnp.sum(own * proj_ref[:, at], axis=0, keepdims=True) * gain_scale


def step_orders(devices):
    steps = [1 << bit for bit in range(devices.bit_length() - 1)]
    half = len(steps) // 2
    even, odd = [], []
    for near, far in zip(steps[:half], steps[half:]):
        even += [near, far]
        odd += [far, near]
    return even + steps[2 * half :], odd + steps[2 * half :]


def shards(streams, layer_out, cotangent, input_cot, gain, projection, static_mix, tanh_scale):
    tokens, count, width = streams.shape
    rows = tokens * count
    dp, tensor = lax.axis_size("dp"), lax.axis_size("tensor")
    full_width = width * tensor
    params = pltpu.CompilerParams(vmem_limit_bytes=VMEM_LIMIT)
    scalars = pl.BlockSpec(memory_space=pltpu.SMEM)

    block = min(STAT_TOKENS, tokens)
    def in_hbm(array):
        return pltpu.with_memory_space_constraint(array, pltpu.HBM)

    def in_vmem(array):
        return pltpu.with_memory_space_constraint(array, pltpu.VMEM)

    streams, cotangent, layer_out, input_cot = map(in_hbm, (streams, cotangent, layer_out, input_cot))
    vmem = pl.BlockSpec(memory_space=pltpu.VMEM)
    hbm = pl.BlockSpec(memory_space=pltpu.HBM)
    stat, hr, gr, g0, w = pl.pallas_call(
        statistics,
        in_specs=[hbm] * 6,
        out_specs=[vmem] * 5,
        out_shape=[
            pltpu.VMEM((2 * PAD, rows), F32),
            pltpu.VMEM((rows, width), BF16),
            pltpu.VMEM((rows, width), BF16),
            pltpu.VMEM((tokens, width), BF16),
            pltpu.VMEM((2 * PAD, width), BF16),
        ],
        scratch_shapes=[
            pltpu.VMEM(streams.shape, BF16),
            pltpu.VMEM(streams.shape, BF16),
            pltpu.VMEM(layer_out.shape, BF16),
            pltpu.VMEM((1, width), F32),
            pltpu.VMEM((COLUMNS, width), F32),
            pltpu.SemaphoreType.DMA((tokens // block, 4)),
            pltpu.SemaphoreType.DMA((2,)),
        ],
        compiler_params=params,
        name="statistics",
    )(streams, cotangent, layer_out, input_cot, in_hbm(gain.reshape(1, width)), in_hbm(projection))

    if tensor == 2:
        stats = (stat, lax.ppermute(stat, "tensor", [(0, 1), (1, 0)]))
    else:
        stats = (lax.psum(stat, "tensor"),)

    group = min(MIX_TOKENS, tokens)
    coef, dw = pl.pallas_call(
        lambda *refs: partials(float(full_width), *refs),
        in_specs=[vmem] * len(stats) + [scalars, vmem],
        out_specs=[vmem] * 2,
        out_shape=[
            pltpu.VMEM((tokens // group, 3 * PAD, group * count), F32),
            pltpu.VMEM((QUARTERS * COLUMNS, width // QUARTERS), F32),
        ],
        compiler_params=params,
        name="partials",
    )(*stats, tanh_scale, in_vmem(hr))

    grads = [jax.ShapeDtypeStruct((tokens, count, width), BF16), jax.ShapeDtypeStruct((tokens, width), BF16)]

    def mixed(first, groups, last, bufs, results):
        own = groups * group
        kept = [pltpu.VMEM((own, count, width), BF16), pltpu.VMEM((own, width), BF16)]
        sems = [pltpu.SemaphoreType.DMA((2,))] * 2
        shape = (grads if bufs or last else []) + ([] if last else kept)
        done = pl.pallas_call(
            lambda *refs: outputs(first, groups, bool(bufs), last, *refs),
            in_specs=[vmem, scalars] + [vmem] * (4 + len(bufs)) + [hbm] * len(results),
            out_specs=([hbm] * 2 if bufs or last else []) + ([] if last else [vmem] * 2),
            out_shape=shape,
            scratch_shapes=(kept if last else []) + sems,
            input_output_aliases={8 + i: i for i in range(len(results))},
            compiler_params=params,
            cost_estimate=pl.CostEstimate(flops=4_000_000_000, bytes_accessed=own * width * 30, transcendentals=0),
            name="outputs",
        )(in_vmem(coef), static_mix, *map(in_vmem, (hr, gr, g0, w, *bufs)), *results)
        return ((), done) if last else (done[-2:], done[:-2])

    sizes = [tokens // group]
    if sizes[0] % WINDOWS == 0 and sizes[0] > WINDOWS:
        each = sizes[0] // WINDOWS
        sizes = [each + 1] + [each] * (WINDOWS - 2) + [each - 1]
    bufs, results, first = (), (), 0
    for index, groups in enumerate(sizes):
        bufs, results = mixed(first, groups, index == len(sizes) - 1, bufs, results)
        first += groups
    stream_grad, out_grad = results

    if dp > 1 and dp & (dp - 1) == 0:
        orders = step_orders(dp)
        for index in range(len(orders[0])):
            pairs = [
                (i * tensor + t, (i ^ orders[t % 2][index]) * tensor + t) for i in range(dp) for t in range(tensor)
            ]
            more = lax.ppermute(dw, ("dp", "tensor"), pairs)
            if index < len(orders[0]) - 1:
                dw = dw + more
    else:
        dw, more = lax.psum(dw, "dp"), jnp.zeros_like(dw)
    all_tokens = tokens * dp
    proj_scale = (float(count) * all_tokens * full_width) ** -0.5
    gain_scale = (float(count) * all_tokens) ** -0.5
    proj_grad, gain_grad = pl.pallas_call(
        lambda *refs: tail(proj_scale, gain_scale, *refs),
        in_specs=[vmem] * 4,
        out_specs=[vmem] * 2,
        out_shape=[jax.ShapeDtypeStruct((COLUMNS, width), F32), jax.ShapeDtypeStruct((1, width), F32)],
        compiler_params=params,
        name="tail",
    )(dw, more, gain.reshape(1, width), projection)
    return (stream_grad, out_grad, proj_grad, gain_grad.reshape(width))


def solution(mesh):
    placed = (
        P("dp", None, "tensor"),
        P("dp", "tensor"),
        P("dp", None, "tensor"),
        P("dp", "tensor"),
        P("tensor"),
        P(None, "tensor"),
        P(),
        P(),
    )
    return jax.shard_map(
        shards,
        mesh=mesh,
        in_specs=placed,
        out_specs=(P("dp", None, "tensor"), P("dp", "tensor"), P(None, "tensor"), P("tensor")),
        check_vma=False,
    )
```

time: 36.7 us -> 30.6 us (0.83)
  Pallas kernels: 23.4 us -> 15.9 us
  waiting for transfers between devices: 1.63 us -> 3.15 us
  starting transfers between devices: 9.27 us -> 10.7 us
  other arithmetic: 1.36 us -> 0.04 us
    pallas_call x5 -> x6, Pallas kernels: 22.2 us -> 14.7 us  [the longest x4 8.11 us: mixed(): pl.pallas_call(lambda *refs: outputs(first, groups, bool(bufs), last, *re...]
    ppermute x4, waiting for transfers between devices: 0.77 us -> 2.29 us  [shards(): more = lax.ppermute(dw, ('dp', 'tensor'), pairs)]
    ppermute x4, starting transfers between devices: 8.71 us -> 10.1 us  [shards(): more = lax.ppermute(dw, ('dp', 'tensor'), pairs)]
    reduce_sum x1 -> x0, other arithmetic: 0.7 us -> none  [shards(): jnp.sum(dw * projection, axis=0) / jnp.sqrt(float(count) * all_tokens)]
    div x1 -> x0, other arithmetic: 0.61 us -> none  [shards(): jnp.sum(dw * projection, axis=0) / jnp.sqrt(float(count) * all_tokens)]
  transfers between devices with their start and end apart: 5 -> 5, of which waited for: 2 -> 5; matrix products, arithmetic and copies ran while one was open for 0% -> 0% of each run, Pallas kernels for 39% -> 27%
where the time goes in v2:
time: 30.6 us; the launch traced here: 30.5 us
  Pallas kernels  15.9 us (52%)
  starting transfers between devices  10.7 us (35%)
  waiting for transfers between devices  3.15 us (10%)
  between operations  0.7 us (2%)
    ppermute x4, starting transfers between devices, shards(): more = lax.ppermute(dw, ('dp', 'tensor'), pairs)  10.1 us
    pallas_call x4, Pallas kernels, mixed(): pl.pallas_call(lambda *refs: outputs(first, groups, bool(bufs), last, *re...  8.11 us
    pallas_call x1, Pallas kernels, shards(): pl.pallas_call(statistics, in_specs=[hbm] * 6, out_specs=[vmem] * 5, out_...  5.85 us
    ppermute x4, waiting for transfers between devices, shards(): more = lax.ppermute(dw, ('dp', 'tensor'), pairs)  2.29 us
    pallas_call x1, Pallas kernels, shards(): pl.pallas_call(lambda *refs: partials(float(full_width), *refs), in_specs...  1.19 us
    ppermute x1, waiting for transfers between devices, shards(): stats = (stat, lax.ppermute(stat, 'tensor', [(0, 1), (1, 0)]))  0.86 us
    pallas_call x1, Pallas kernels, shards(): pl.pallas_call(lambda *refs: tail(proj_scale, gain_scale, *refs), in_spec...  0.73 us
  transfers between devices with their start and end apart: 5, of which 5 were waited for; matrix products, arithmetic and copies ran while one was open for 0% of the time, Pallas kernels for 27%

profile of v2, /device:TPU:0, one launch (start us, length us, event | category | flops | bytes accessed | tf_op | source)
XLA Modules:
  0.0 30.5 jit_solution(3658742806353100570)
XLA Ops:
  0.6 0.0 copy-start.3
  0.6 5.8 %statistics.1 = (f32[16,512]{1,0:T(8,128)S(1)}, bf16[512,4096]{1,0:T(8,128)(2,1)S(1)}, bf16[512,4096]{1,0:T(8,128)(2,1)S(1)}, bf16[128,4096]{1,0:T(8,128)(2,1)S(1)}, bf16[16,4096]{1,0:T(8,128)(2,1)S(1)}) custom-call(bf16[128,4,4096]{2,1,0:T(4,128)(2,1)} %h_hbm.1, bf16[128,4,4096]{2,1,0:T(4,128)(2,1)} %g_hbm.1, bf16[128,4096]{1,0:T(8,128)(2,1)} %y_hbm.1, ...), custom_call_target="tpu_custom_call" | custom-call | tf_op jit(solution)/shard_map/statistics/pallas_call | solution.py:245
  6.5 0.0 copy-start.2
  6.5 0.6 %collective-permute-start = (f32[16,512]{1,0:T(8,128)S(1)}, f32[16,512]{1,0:T(8,128)S(1)}, u32[]{:S(2)}, u32[]{:S(2)}) collective-permute-start(f32[16,512]{1,0:T(8,128)S(1)} %get-tuple-element.25.refs_0_), channel_id=1, source_target_pairs={{0,1},{1,0},{2,3},{3,2},{4,5},{5,4},{6,7},{7,6},{8,9},{9,8},{10,11... | collective-permute-start | bytes 98312 | tf_op jit(solution)/shard_map/ppermute | solution.py:270
  7.1 0.9 %collective-permute-done.refs_1_ = f32[16,512]{1,0:T(8,128)S(1)} collective-permute-done((f32[16,512]{1,0:T(8,128)S(1)}, f32[16,512]{1,0:T(8,128)S(1)}, u32[]{:S(2)}, u32[]{:S(2)}) %collective-permute-start) | collective-permute-done | bytes 32800 | tf_op jit(solution)/shard_map/ppermute | solution.py:270
  7.9 0.0 copy-done.3
  7.9 1.2 %partials.1 = (f32[8,24,64]{2,1,0:T(8,128)S(1)}, f32[24,1024]{1,0:T(8,128)S(1)}) custom-call(f32[16,512]{1,0:T(8,128)S(1)} %get-tuple-element.25.refs_0_, f32[16,512]{1,0:T(8,128)S(1)} %collective-permute-done.refs_1_, f32[3]{0:T(128)S(1)} %copy-done.3, bf16[512,4096]{1,0:T(8,128)(2,1)S(1)} %get-tuple-element.26.refs_3_.refs_2_), custom_call_target="tpu_custom_call" | custom-call | tf_op jit(solution)/shard_map/partials/pallas_call | solution.py:275
  9.1 2.8 %collective-permute-start.1 = (f32[24,1024]{1,0:T(8,128)S(1)}, f32[24,1024]{1,0:T(8,128)S(1)}, u32[]{:S(2)}, u32[]{:S(2)}) collective-permute-start(f32[24,1024]{1,0:T(8,128)S(1)} %get-tuple-element.43), channel_id=1, source_target_pairs={{0,2},{1,9},{2,0},{3,11},{4,6},{5,13},{6,4},{7,15},{8,10},{9,1},{1... | collective-permute-start | bytes 294920 | tf_op jit(solution)/shard_map/ppermute | solution.py:323
  12.0 0.0 copy-done.2
  12.0 2.2 %outputs.4 = (bf16[48,4,4096]{2,1,0:T(4,128)(2,1)S(1)}, bf16[48,4096]{1,0:T(8,128)(2,1)S(1)}) custom-call(f32[8,24,64]{2,1,0:T(8,128)S(1)} %get-tuple-element.27.refs_0_, f32[4,6]{1,0:T(4,128)S(1)} %copy-done.2, bf16[512,4096]{1,0:T(8,128)(2,1)S(1)} %get-tuple-element.26.refs_3_.refs_2_, bf16[512,4096]{1,0:T(8,128)(2,1)S(1)} %get-tuple-element.28.refs_3_, ...), custom_call_target="tpu_custom_call" | custom-call | flops 4000000000 | bytes 5898240 | tf_op jit(solution)/shard_map/outputs/pallas_call | solution.py:294
  14.2 0.4 %collective-permute-done.1 = f32[24,1024]{1,0:T(8,128)S(1)} collective-permute-done((f32[24,1024]{1,0:T(8,128)S(1)}, f32[24,1024]{1,0:T(8,128)S(1)}, u32[]{:S(2)}, u32[]{:S(2)}) %collective-permute-start.1) | collective-permute-done | bytes 98336 | tf_op jit(solution)/shard_map/ppermute | solution.py:323
  14.6 2.2 %collective-permute-start.2 = (f32[24,1024]{1,0:T(8,128)S(1)}, f32[24,1024]{1,0:T(8,128)S(1)}, u32[]{:S(2)}, u32[]{:S(2)}) collective-permute-start(f32[24,1024]{1,0:T(8,128)S(1)} %add.9), channel_id=1, source_target_pairs={{0,8},{1,3},{2,10},{3,1},{4,12},{5,7},{6,14},{7,5},{8,0},{9,11},{1... | collective-permute-start | bytes 294920 | tf_op jit(solution)/shard_map/ppermute | solution.py:323
  16.7 1.9 %outputs.5 = (bf16[128,4,4096]{2,1,0:T(4,128)(2,1)}, bf16[128,4096]{1,0:T(8,128)(2,1)}, bf16[32,4,4096]{2,1,0:T(4,128)(2,1)S(1)}, bf16[32,4096]{1,0:T(8,128)(2,1)S(1)}) custom-call(f32[8,24,64]{2,1,0:T(8,128)S(1)} %get-tuple-element.27.refs_0_, f32[4,6]{1,0:T(4,128)S(1)} %copy-done.2, bf16[512,4096]{1,0:T(8,128)(2,1)S(1)} %get-tuple-element.26.refs_3_.refs_2_, ...), custom_call_target="tpu_custom_call" | custom-call | flops 4000000000 | bytes 3932160 | tf_op jit(solution)/shard_map/outputs/pallas_call | solution.py:294
  18.6 0.7 %collective-permute-done.2 = f32[24,1024]{1,0:T(8,128)S(1)} collective-permute-done((f32[24,1024]{1,0:T(8,128)S(1)}, f32[24,1024]{1,0:T(8,128)S(1)}, u32[]{:S(2)}, u32[]{:S(2)}) %collective-permute-start.2) | collective-permute-done | bytes 98336 | tf_op jit(solution)/shard_map/ppermute | solution.py:323
  19.4 2.0 %collective-permute-start.3 = (f32[24,1024]{1,0:T(8,128)S(1)}, f32[24,1024]{1,0:T(8,128)S(1)}, u32[]{:S(2)}, u32[]{:S(2)}) collective-permute-start(f32[24,1024]{1,0:T(8,128)S(1)} %add.10), channel_id=1, source_target_pairs={{0,4},{1,17},{2,6},{3,19},{4,0},{5,21},{6,2},{7,23},{8,12},{9,25},... | collective-permute-start | bytes 294920 | tf_op jit(solution)/shard_map/ppermute | solution.py:323
  21.4 1.8 %outputs.6 = (bf16[128,4,4096]{2,1,0:T(4,128)(2,1)}, bf16[128,4096]{1,0:T(8,128)(2,1)}, bf16[32,4,4096]{2,1,0:T(4,128)(2,1)S(1)}, bf16[32,4096]{1,0:T(8,128)(2,1)S(1)}) custom-call(f32[8,24,64]{2,1,0:T(8,128)S(1)} %get-tuple-element.27.refs_0_, f32[4,6]{1,0:T(4,128)S(1)} %copy-done.2, ...), custom_call_target="tpu_custom_call", output_to_operand_aliasing={{0}: (8, {}), {1}: (9, {})} | custom-call | flops 4000000000 | bytes 3932160 | tf_op jit(solution)/shard_map/outputs/pallas_call | solution.py:294
  23.2 0.8 %collective-permute-done.3 = f32[24,1024]{1,0:T(8,128)S(1)} collective-permute-done((f32[24,1024]{1,0:T(8,128)S(1)}, f32[24,1024]{1,0:T(8,128)S(1)}, u32[]{:S(2)}, u32[]{:S(2)}) %collective-permute-start.3) | collective-permute-done | bytes 98336 | tf_op jit(solution)/shard_map/ppermute | solution.py:323
  24.1 3.1 %collective-permute-start.4 = (f32[24,1024]{1,0:T(8,128)S(1)}, f32[24,1024]{1,0:T(8,128)S(1)}, u32[]{:S(2)}, u32[]{:S(2)}) collective-permute-start(f32[24,1024]{1,0:T(8,128)S(1)} %add.11.refs_0_), channel_id=1, source_target_pairs={{0,16},{1,5},{2,18},{3,7},{4,20},{5,1},{6,22},{7,3},{8,24},{9,13},... | collective-permute-start | bytes 294920 | tf_op jit(solution)/shard_map/ppermute | solution.py:323
  27.2 0.0 copy-start
  27.2 0.0 copy-start.1
  27.2 2.3 %outputs.7 = (bf16[128,4,4096]{2,1,0:T(4,128)(2,1)}, bf16[128,4096]{1,0:T(8,128)(2,1)}) custom-call(f32[8,24,64]{2,1,0:T(8,128)S(1)} %get-tuple-element.27.refs_0_, f32[4,6]{1,0:T(4,128)S(1)} %copy-done.2, bf16[512,4096]{1,0:T(8,128)(2,1)S(1)} %get-tuple-element.26.refs_3_.refs_2_, ...), custom_call_target="tpu_custom_call", output_to_operand_aliasing={{0}: (8, {}), {1}: (9, {})} | custom-call | flops 4000000000 | bytes 1966080 | tf_op jit(solution)/shard_map/outputs/pallas_call | solution.py:294
  29.4 0.3 %collective-permute-done.4.refs_1_ = f32[24,1024]{1,0:T(8,128)S(1)} collective-permute-done((f32[24,1024]{1,0:T(8,128)S(1)}, f32[24,1024]{1,0:T(8,128)S(1)}, u32[]{:S(2)}, u32[]{:S(2)}) %collective-permute-start.4) | collective-permute-done | bytes 98336 | tf_op jit(solution)/shard_map/ppermute | solution.py:323
  29.8 0.0 copy-done
  29.8 0.0 copy-done.1
  29.8 0.7 %tail.1 = (f32[6,4096]{1,0:T(8,128)}, f32[1,4096]{1,0:T(1,128)}) custom-call(f32[24,1024]{1,0:T(8,128)S(1)} %add.11.refs_0_, f32[24,1024]{1,0:T(8,128)S(1)} %collective-permute-done.4.refs_1_, f32[1,4096]{1,0:T(1,128)S(1)} %bitcast.3, f32[6,4096]{1,0:T(8,128)S(1)} %copy-done), custom_call_target="tpu_custom_call" | custom-call | tf_op jit(solution)/shard_map/tail/pallas_call | solution.py:331
  (3 shorter events, 0.0 us)
Async XLA Ops:
  0.6 7.3 %copy-start.3 = (f32[3]{0:T(128)S(1)}, f32[3]{0:T(128)}, u32[]{:S(2)}) copy-start(f32[3]{0:T(128)} %refs_2_.1) | copy-start | bytes 40
  6.5 5.5 %copy-start.2 = (f32[4,6]{1,0:T(4,128)S(1)}, f32[4,6]{1,0:T(4,128)}, u32[]{:S(2)}) copy-start(f32[4,6]{1,0:T(4,128)} %refs_1_.7) | copy-start | bytes 292
  6.5 1.4 %collective-permute-start = (f32[16,512]{1,0:T(8,128)S(1)}, f32[16,512]{1,0:T(8,128)S(1)}, u32[]{:S(2)}, u32[]{:S(2)}) collective-permute-start(f32[16,512]{1,0:T(8,128)S(1)} %get-tuple-element.25.refs_0_), channel_id=1, source_target_pairs={{0,1},{1,0},{2,3},{3,2},{4,5},{5,4},{6,7},{7,6},{8,9},{9,8},{10,11... | collective-permute-start | bytes 98312 | tf_op jit(solution)/shard_map/ppermute | solution.py:270
  9.1 5.4 %collective-permute-start.1 = (f32[24,1024]{1,0:T(8,128)S(1)}, f32[24,1024]{1,0:T(8,128)S(1)}, u32[]{:S(2)}, u32[]{:S(2)}) collective-permute-start(f32[24,1024]{1,0:T(8,128)S(1)} %get-tuple-element.43), channel_id=1, source_target_pairs={{0,2},{1,9},{2,0},{3,11},{4,6},{5,13},{6,4},{7,15},{8,10},{9,1},{1... | collective-permute-start | bytes 294920 | tf_op jit(solution)/shard_map/ppermute | solution.py:323
  14.6 4.8 %collective-permute-start.2 = (f32[24,1024]{1,0:T(8,128)S(1)}, f32[24,1024]{1,0:T(8,128)S(1)}, u32[]{:S(2)}, u32[]{:S(2)}) collective-permute-start(f32[24,1024]{1,0:T(8,128)S(1)} %add.9), channel_id=1, source_target_pairs={{0,8},{1,3},{2,10},{3,1},{4,12},{5,7},{6,14},{7,5},{8,0},{9,11},{1... | collective-permute-start | bytes 294920 | tf_op jit(solution)/shard_map/ppermute | solution.py:323
  19.4 4.7 %collective-permute-start.3 = (f32[24,1024]{1,0:T(8,128)S(1)}, f32[24,1024]{1,0:T(8,128)S(1)}, u32[]{:S(2)}, u32[]{:S(2)}) collective-permute-start(f32[24,1024]{1,0:T(8,128)S(1)} %add.10), channel_id=1, source_target_pairs={{0,4},{1,17},{2,6},{3,19},{4,0},{5,21},{6,2},{7,23},{8,12},{9,25},... | collective-permute-start | bytes 294920 | tf_op jit(solution)/shard_map/ppermute | solution.py:323
  24.1 5.7 %collective-permute-start.4 = (f32[24,1024]{1,0:T(8,128)S(1)}, f32[24,1024]{1,0:T(8,128)S(1)}, u32[]{:S(2)}, u32[]{:S(2)}) collective-permute-start(f32[24,1024]{1,0:T(8,128)S(1)} %add.11.refs_0_), channel_id=1, source_target_pairs={{0,16},{1,5},{2,18},{3,7},{4,20},{5,1},{6,22},{7,3},{8,24},{9,13},... | collective-permute-start | bytes 294920 | tf_op jit(solution)/shard_map/ppermute | solution.py:323
  27.2 2.6 %copy-start = (f32[6,4096]{1,0:T(8,128)S(1)}, f32[6,4096]{1,0:T(8,128)}, u32[]{:S(2)}) copy-start(f32[6,4096]{1,0:T(8,128)} %refs_3_.1) | copy-start | bytes 294916
  27.2 2.6 %copy-start.1 = (f32[4096]{0:T(1024)S(1)}, f32[4096]{0:T(1024)}, u32[]{:S(2)}) copy-start(f32[4096]{0:T(1024)} %param.12) | copy-start | bytes 49156

commit v3 on v2

--- a/solution.py
+++ b/solution.py
@@ -14,7 +14,7 @@
 STAT_TOKENS = 32
 MIX_TOKENS = 16
 WINDOWS = 4
-AHEAD = 2
+DEPTHS = 4
 VMEM_LIMIT = 30 * 1024 * 1024
 
 
@@ -61,9 +61,9 @@
 
     for copy in weights:
         copy.start()
-    for block in range(min(AHEAD, blocks)):
+    for block in range(blocks):
         for copy in copies(block):
-            copy.start(priority=block % 2)
+            copy.start(priority=min(block, 1))
     for copy in weights:
         copy.wait()
     high, low = split(gain_buf[...] * proj_buf[...])
@@ -75,11 +75,6 @@
         for copy in copies(block):
             copy.wait()
 
-        @pl.when(block + AHEAD < blocks)
-        def _():
-            for copy in copies(block + AHEAD):
-                copy.start(priority=1)
-
         statistics_of(block, tokens, stat_ref, hr_ref, gr_ref, g0_ref, w_ref, h_buf, g_buf, y_buf)
 
 
@@ -88,15 +83,18 @@
     rows = tokens * streams
     at = pl.ds(pl.multiple_of(block * tokens, tokens), tokens)
     own = pl.ds(pl.multiple_of(block * rows, rows), rows)
-    hr_ref[own, :] = h_buf[at].reshape(rows, width)
-    gr_ref[own, :] = g_buf[at].reshape(rows, width)
-    h = hr_ref[own, :]
-    left = jnp.concatenate([gr_ref[own, :], g0_ref[at, :], w_ref[...]], axis=0)
-    product = dot(left, jnp.concatenate([h, y_buf[at, :]], axis=0), (1, 1))
+    product = 0.0
+    depth = width // DEPTHS
+    for start in range(0, width, depth):
+        part = pl.ds(start, depth)
+        hr_ref[own, part] = h_buf[at, :, part].reshape(rows, depth)
+        gr_ref[own, part] = g_buf[at, :, part].reshape(rows, depth)
+        left = jnp.concatenate([gr_ref[own, part], g0_ref[at, part], w_ref[:, part]], axis=0)
+        product = product + dot(left, jnp.concatenate([hr_ref[own, part], y_buf[at, part]], axis=0), (1, 1))
     lanes = 128
     square = jnp.zeros((rows, lanes), F32)
     for start in range(0, width, lanes):
-        part = h[:, start : start + lanes].astype(F32)
+        part = hr_ref[own, pl.ds(start, lanes)].astype(F32)
         square = square + part * part
     square = jnp.sum(square.T, axis=0, keepdims=True)
     line, token = iota((rows, rows), 0), iota((rows, rows), 1) // streams

time: 30.6 us -> 29.8 us (0.974)
  Pallas kernels: 15.9 us -> 15.1 us
    pallas_call x1, Pallas kernels: 5.85 us -> 5.04 us  [shards(): pl.pallas_call(statistics, in_specs=[hbm] * 6, out_specs=[vmem] * 5, out_...]
where the time goes in v3:
time: 29.8 us; the launch traced here: 29.7 us
  Pallas kernels  15.1 us (51%)
  starting transfers between devices  10.7 us (36%)
  waiting for transfers between devices  3.14 us (11%)
  between operations  0.7 us (2%)
    ppermute x4, starting transfers between devices, shards(): more = lax.ppermute(dw, ('dp', 'tensor'), pairs)  10.1 us
    pallas_call x4, Pallas kernels, mixed(): pl.pallas_call(lambda *refs: outputs(first, groups, bool(bufs), last, *re...  8.11 us
    pallas_call x1, Pallas kernels, shards(): pl.pallas_call(statistics, in_specs=[hbm] * 6, out_specs=[vmem] * 5, out_...  5.04 us
    ppermute x4, waiting for transfers between devices, shards(): more = lax.ppermute(dw, ('dp', 'tensor'), pairs)  2.28 us
    pallas_call x1, Pallas kernels, shards(): pl.pallas_call(lambda *refs: partials(float(full_width), *refs), in_specs...  1.19 us
    ppermute x1, waiting for transfers between devices, shards(): stats = (stat, lax.ppermute(stat, 'tensor', [(0, 1), (1, 0)]))  0.86 us
    pallas_call x1, Pallas kernels, shards(): pl.pallas_call(lambda *refs: tail(proj_scale, gain_scale, *refs), in_spec...  0.73 us
  transfers between devices with their start and end apart: 5, of which 5 were waited for; matrix products, arithmetic and copies ran while one was open for 0% of the time, Pallas kernels for 27%

profile of v3, /device:TPU:0, one launch (start us, length us, event | category | flops | bytes accessed | tf_op | source)
XLA Modules:
  0.0 29.7 jit_solution(14832943643789435253)
XLA Ops:
  0.6 0.0 copy-start.3
  0.6 5.0 %statistics.1 = (f32[16,512]{1,0:T(8,128)S(1)}, bf16[512,4096]{1,0:T(8,128)(2,1)S(1)}, bf16[512,4096]{1,0:T(8,128)(2,1)S(1)}, bf16[128,4096]{1,0:T(8,128)(2,1)S(1)}, bf16[16,4096]{1,0:T(8,128)(2,1)S(1)}) custom-call(bf16[128,4,4096]{2,1,0:T(4,128)(2,1)} %h_hbm.1, bf16[128,4,4096]{2,1,0:T(4,128)(2,1)} %g_hbm.1, bf16[128,4096]{1,0:T(8,128)(2,1)} %y_hbm.1, ...), custom_call_target="tpu_custom_call" | custom-call | tf_op jit(solution)/shard_map/statistics/pallas_call | solution.py:243
  5.7 0.0 copy-start.2
  5.7 0.6 %collective-permute-start = (f32[16,512]{1,0:T(8,128)S(1)}, f32[16,512]{1,0:T(8,128)S(1)}, u32[]{:S(2)}, u32[]{:S(2)}) collective-permute-start(f32[16,512]{1,0:T(8,128)S(1)} %get-tuple-element.25.refs_0_), channel_id=1, source_target_pairs={{0,1},{1,0},{2,3},{3,2},{4,5},{5,4},{6,7},{7,6},{8,9},{9,8},{10,11... | collective-permute-start | bytes 98312 | tf_op jit(solution)/shard_map/ppermute | solution.py:268
  6.3 0.9 %collective-permute-done.refs_1_ = f32[16,512]{1,0:T(8,128)S(1)} collective-permute-done((f32[16,512]{1,0:T(8,128)S(1)}, f32[16,512]{1,0:T(8,128)S(1)}, u32[]{:S(2)}, u32[]{:S(2)}) %collective-permute-start) | collective-permute-done | bytes 32800 | tf_op jit(solution)/shard_map/ppermute | solution.py:268
  7.1 0.0 copy-done.3
  7.1 1.2 %partials.1 = (f32[8,24,64]{2,1,0:T(8,128)S(1)}, f32[24,1024]{1,0:T(8,128)S(1)}) custom-call(f32[16,512]{1,0:T(8,128)S(1)} %get-tuple-element.25.refs_0_, f32[16,512]{1,0:T(8,128)S(1)} %collective-permute-done.refs_1_, f32[3]{0:T(128)S(1)} %copy-done.3, bf16[512,4096]{1,0:T(8,128)(2,1)S(1)} %get-tuple-element.26.refs_3_.refs_2_), custom_call_target="tpu_custom_call" | custom-call | tf_op jit(solution)/shard_map/partials/pallas_call | solution.py:273
  8.3 2.8 %collective-permute-start.1 = (f32[24,1024]{1,0:T(8,128)S(1)}, f32[24,1024]{1,0:T(8,128)S(1)}, u32[]{:S(2)}, u32[]{:S(2)}) collective-permute-start(f32[24,1024]{1,0:T(8,128)S(1)} %get-tuple-element.43), channel_id=1, source_target_pairs={{0,2},{1,9},{2,0},{3,11},{4,6},{5,13},{6,4},{7,15},{8,10},{9,1},{1... | collective-permute-start | bytes 294920 | tf_op jit(solution)/shard_map/ppermute | solution.py:321
  11.2 0.0 copy-done.2
  11.2 2.2 %outputs.4 = (bf16[48,4,4096]{2,1,0:T(4,128)(2,1)S(1)}, bf16[48,4096]{1,0:T(8,128)(2,1)S(1)}) custom-call(f32[8,24,64]{2,1,0:T(8,128)S(1)} %get-tuple-element.27.refs_0_, f32[4,6]{1,0:T(4,128)S(1)} %copy-done.2, bf16[512,4096]{1,0:T(8,128)(2,1)S(1)} %get-tuple-element.26.refs_3_.refs_2_, bf16[512,4096]{1,0:T(8,128)(2,1)S(1)} %get-tuple-element.28.refs_3_, ...), custom_call_target="tpu_custom_call" | custom-call | flops 4000000000 | bytes 5898240 | tf_op jit(solution)/shard_map/outputs/pallas_call | solution.py:292
  13.4 0.4 %collective-permute-done.1 = f32[24,1024]{1,0:T(8,128)S(1)} collective-permute-done((f32[24,1024]{1,0:T(8,128)S(1)}, f32[24,1024]{1,0:T(8,128)S(1)}, u32[]{:S(2)}, u32[]{:S(2)}) %collective-permute-start.1) | collective-permute-done | bytes 98336 | tf_op jit(solution)/shard_map/ppermute | solution.py:321
  13.8 2.2 %collective-permute-start.2 = (f32[24,1024]{1,0:T(8,128)S(1)}, f32[24,1024]{1,0:T(8,128)S(1)}, u32[]{:S(2)}, u32[]{:S(2)}) collective-permute-start(f32[24,1024]{1,0:T(8,128)S(1)} %add.9), channel_id=1, source_target_pairs={{0,8},{1,3},{2,10},{3,1},{4,12},{5,7},{6,14},{7,5},{8,0},{9,11},{1... | collective-permute-start | bytes 294920 | tf_op jit(solution)/shard_map/ppermute | solution.py:321
  15.9 1.9 %outputs.5 = (bf16[128,4,4096]{2,1,0:T(4,128)(2,1)}, bf16[128,4096]{1,0:T(8,128)(2,1)}, bf16[32,4,4096]{2,1,0:T(4,128)(2,1)S(1)}, bf16[32,4096]{1,0:T(8,128)(2,1)S(1)}) custom-call(f32[8,24,64]{2,1,0:T(8,128)S(1)} %get-tuple-element.27.refs_0_, f32[4,6]{1,0:T(4,128)S(1)} %copy-done.2, bf16[512,4096]{1,0:T(8,128)(2,1)S(1)} %get-tuple-element.26.refs_3_.refs_2_, ...), custom_call_target="tpu_custom_call" | custom-call | flops 4000000000 | bytes 3932160 | tf_op jit(solution)/shard_map/outputs/pallas_call | solution.py:292
  17.8 0.7 %collective-permute-done.2 = f32[24,1024]{1,0:T(8,128)S(1)} collective-permute-done((f32[24,1024]{1,0:T(8,128)S(1)}, f32[24,1024]{1,0:T(8,128)S(1)}, u32[]{:S(2)}, u32[]{:S(2)}) %collective-permute-start.2) | collective-permute-done | bytes 98336 | tf_op jit(solution)/shard_map/ppermute | solution.py:321
  18.5 2.0 %collective-permute-start.3 = (f32[24,1024]{1,0:T(8,128)S(1)}, f32[24,1024]{1,0:T(8,128)S(1)}, u32[]{:S(2)}, u32[]{:S(2)}) collective-permute-start(f32[24,1024]{1,0:T(8,128)S(1)} %add.10), channel_id=1, source_target_pairs={{0,4},{1,17},{2,6},{3,19},{4,0},{5,21},{6,2},{7,23},{8,12},{9,25},... | collective-permute-start | bytes 294920 | tf_op jit(solution)/shard_map/ppermute | solution.py:321
  20.6 1.8 %outputs.6 = (bf16[128,4,4096]{2,1,0:T(4,128)(2,1)}, bf16[128,4096]{1,0:T(8,128)(2,1)}, bf16[32,4,4096]{2,1,0:T(4,128)(2,1)S(1)}, bf16[32,4096]{1,0:T(8,128)(2,1)S(1)}) custom-call(f32[8,24,64]{2,1,0:T(8,128)S(1)} %get-tuple-element.27.refs_0_, f32[4,6]{1,0:T(4,128)S(1)} %copy-done.2, ...), custom_call_target="tpu_custom_call", output_to_operand_aliasing={{0}: (8, {}), {1}: (9, {})} | custom-call | flops 4000000000 | bytes 3932160 | tf_op jit(solution)/shard_map/outputs/pallas_call | solution.py:292
  22.4 0.8 %collective-permute-done.3 = f32[24,1024]{1,0:T(8,128)S(1)} collective-permute-done((f32[24,1024]{1,0:T(8,128)S(1)}, f32[24,1024]{1,0:T(8,128)S(1)}, u32[]{:S(2)}, u32[]{:S(2)}) %collective-permute-start.3) | collective-permute-done | bytes 98336 | tf_op jit(solution)/shard_map/ppermute | solution.py:321
  23.2 3.1 %collective-permute-start.4 = (f32[24,1024]{1,0:T(8,128)S(1)}, f32[24,1024]{1,0:T(8,128)S(1)}, u32[]{:S(2)}, u32[]{:S(2)}) collective-permute-start(f32[24,1024]{1,0:T(8,128)S(1)} %add.11.refs_0_), channel_id=1, source_target_pairs={{0,16},{1,5},{2,18},{3,7},{4,20},{5,1},{6,22},{7,3},{8,24},{9,13},... | collective-permute-start | bytes 294920 | tf_op jit(solution)/shard_map/ppermute | solution.py:321
  26.4 0.0 copy-start
  26.4 0.0 copy-start.1
  26.4 2.3 %outputs.7 = (bf16[128,4,4096]{2,1,0:T(4,128)(2,1)}, bf16[128,4096]{1,0:T(8,128)(2,1)}) custom-call(f32[8,24,64]{2,1,0:T(8,128)S(1)} %get-tuple-element.27.refs_0_, f32[4,6]{1,0:T(4,128)S(1)} %copy-done.2, bf16[512,4096]{1,0:T(8,128)(2,1)S(1)} %get-tuple-element.26.refs_3_.refs_2_, ...), custom_call_target="tpu_custom_call", output_to_operand_aliasing={{0}: (8, {}), {1}: (9, {})} | custom-call | flops 4000000000 | bytes 1966080 | tf_op jit(solution)/shard_map/outputs/pallas_call | solution.py:292
  28.6 0.3 %collective-permute-done.4.refs_1_ = f32[24,1024]{1,0:T(8,128)S(1)} collective-permute-done((f32[24,1024]{1,0:T(8,128)S(1)}, f32[24,1024]{1,0:T(8,128)S(1)}, u32[]{:S(2)}, u32[]{:S(2)}) %collective-permute-start.4) | collective-permute-done | bytes 98336 | tf_op jit(solution)/shard_map/ppermute | solution.py:321
  28.9 0.0 copy-done
  28.9 0.0 copy-done.1
  29.0 0.7 %tail.1 = (f32[6,4096]{1,0:T(8,128)}, f32[1,4096]{1,0:T(1,128)}) custom-call(f32[24,1024]{1,0:T(8,128)S(1)} %add.11.refs_0_, f32[24,1024]{1,0:T(8,128)S(1)} %collective-permute-done.4.refs_1_, f32[1,4096]{1,0:T(1,128)S(1)} %bitcast.3, f32[6,4096]{1,0:T(8,128)S(1)} %copy-done), custom_call_target="tpu_custom_call" | custom-call | tf_op jit(solution)/shard_map/tail/pallas_call | solution.py:329
  (3 shorter events, 0.0 us)
Async XLA Ops:
  0.6 6.5 %copy-start.3 = (f32[3]{0:T(128)S(1)}, f32[3]{0:T(128)}, u32[]{:S(2)}) copy-start(f32[3]{0:T(128)} %refs_2_.1) | copy-start | bytes 40
  5.7 5.5 %copy-start.2 = (f32[4,6]{1,0:T(4,128)S(1)}, f32[4,6]{1,0:T(4,128)}, u32[]{:S(2)}) copy-start(f32[4,6]{1,0:T(4,128)} %refs_1_.7) | copy-start | bytes 292
  5.7 1.4 %collective-permute-start = (f32[16,512]{1,0:T(8,128)S(1)}, f32[16,512]{1,0:T(8,128)S(1)}, u32[]{:S(2)}, u32[]{:S(2)}) collective-permute-start(f32[16,512]{1,0:T(8,128)S(1)} %get-tuple-element.25.refs_0_), channel_id=1, source_target_pairs={{0,1},{1,0},{2,3},{3,2},{4,5},{5,4},{6,7},{7,6},{8,9},{9,8},{10,11... | collective-permute-start | bytes 98312 | tf_op jit(solution)/shard_map/ppermute | solution.py:268
  8.3 5.4 %collective-permute-start.1 = (f32[24,1024]{1,0:T(8,128)S(1)}, f32[24,1024]{1,0:T(8,128)S(1)}, u32[]{:S(2)}, u32[]{:S(2)}) collective-permute-start(f32[24,1024]{1,0:T(8,128)S(1)} %get-tuple-element.43), channel_id=1, source_target_pairs={{0,2},{1,9},{2,0},{3,11},{4,6},{5,13},{6,4},{7,15},{8,10},{9,1},{1... | collective-permute-start | bytes 294920 | tf_op jit(solution)/shard_map/ppermute | solution.py:321
  13.8 4.8 %collective-permute-start.2 = (f32[24,1024]{1,0:T(8,128)S(1)}, f32[24,1024]{1,0:T(8,128)S(1)}, u32[]{:S(2)}, u32[]{:S(2)}) collective-permute-start(f32[24,1024]{1,0:T(8,128)S(1)} %add.9), channel_id=1, source_target_pairs={{0,8},{1,3},{2,10},{3,1},{4,12},{5,7},{6,14},{7,5},{8,0},{9,11},{1... | collective-permute-start | bytes 294920 | tf_op jit(solution)/shard_map/ppermute | solution.py:321
  18.5 4.7 %collective-permute-start.3 = (f32[24,1024]{1,0:T(8,128)S(1)}, f32[24,1024]{1,0:T(8,128)S(1)}, u32[]{:S(2)}, u32[]{:S(2)}) collective-permute-start(f32[24,1024]{1,0:T(8,128)S(1)} %add.10), channel_id=1, source_target_pairs={{0,4},{1,17},{2,6},{3,19},{4,0},{5,21},{6,2},{7,23},{8,12},{9,25},... | collective-permute-start | bytes 294920 | tf_op jit(solution)/shard_map/ppermute | solution.py:321
  23.2 5.7 %collective-permute-start.4 = (f32[24,1024]{1,0:T(8,128)S(1)}, f32[24,1024]{1,0:T(8,128)S(1)}, u32[]{:S(2)}, u32[]{:S(2)}) collective-permute-start(f32[24,1024]{1,0:T(8,128)S(1)} %add.11.refs_0_), channel_id=1, source_target_pairs={{0,16},{1,5},{2,18},{3,7},{4,20},{5,1},{6,22},{7,3},{8,24},{9,13},... | collective-permute-start | bytes 294920 | tf_op jit(solution)/shard_map/ppermute | solution.py:321
  26.4 2.6 %copy-start = (f32[6,4096]{1,0:T(8,128)S(1)}, f32[6,4096]{1,0:T(8,128)}, u32[]{:S(2)}) copy-start(f32[6,4096]{1,0:T(8,128)} %refs_3_.1) | copy-start | bytes 294916
  26.4 2.6 %copy-start.1 = (f32[4096]{0:T(1024)S(1)}, f32[4096]{0:T(1024)}, u32[]{:S(2)}) copy-start(f32[4096]{0:T(1024)} %param.12) | copy-start | bytes 49156

commit v4 on v3

--- a/solution.py
+++ b/solution.py
@@ -40,8 +40,35 @@
     return picked.astype(F32)
 
 
+def column_of(row, count):
+    wanted = jnp.minimum(iota((PAD, count), 0), count - 1)
+    return jnp.sum(jnp.where(iota((PAD, count), 1) == wanted, row, 0.0), axis=1, keepdims=True)
+
+
 def statistics(
-    h_hbm, g_hbm, y_hbm, g0_hbm, gain_hbm, proj_hbm, stat_ref, hr_ref, gr_ref, g0_ref, w_ref, h_buf, g_buf, y_buf, gain_buf, proj_buf, sems, more_sems
+    h_hbm,
+    g_hbm,
+    y_hbm,
+    g0_hbm,
+    gain_hbm,
+    proj_hbm,
+    mix_hbm,
+    scale_hbm,
+    stat_ref,
+    hr_ref,
+    gr_ref,
+    g0_ref,
+    w_ref,
+    table_ref,
+    h_buf,
+    g_buf,
+    y_buf,
+    gain_buf,
+    proj_buf,
+    mix_buf,
+    scale_buf,
+    sems,
+    more_sems,
 ):
     total, streams, width = h_hbm.shape
     blocks = sems.shape[0]
@@ -49,6 +76,8 @@
     weights = [
         pltpu.make_async_copy(gain_hbm, gain_buf, more_sems.at[0]),
         pltpu.make_async_copy(proj_hbm, proj_buf, more_sems.at[1]),
+        pltpu.make_async_copy(mix_hbm, mix_buf, more_sems.at[2]),
+        pltpu.make_async_copy(scale_hbm, scale_buf, more_sems.at[3]),
     ]
 
     def copies(block):
@@ -69,6 +98,14 @@
     high, low = split(gain_buf[...] * proj_buf[...])
     none = jnp.zeros((PAD - COLUMNS, width), F32)
     w_ref[...] = jnp.concatenate([high.astype(F32), none, low.astype(F32), none], axis=0).astype(BF16)
+
+    lanes = table_ref.shape[1]
+    stream = iota((PAD, lanes), 1) % streams
+    static = jnp.zeros((PAD, lanes), F32)
+    for j in range(streams):
+        static = jnp.where(stream == j, column_of(mix_buf[j : j + 1, :], COLUMNS), static)
+    table_ref[:PAD] = static
+    table_ref[PAD:] = jnp.broadcast_to(column_of(scale_buf[...], scale_buf.shape[1]), (PAD, lanes))
 
     @pl.loop(0, blocks)
     def _(block):
@@ -111,13 +148,8 @@
     stat_ref[:, own] = jnp.concatenate([beta, alpha, folded, square, jnp.zeros_like(square), lin], axis=0)
 
 
-def scales_of(scale_ref, shape):
-    row = iota(shape, 0)
-    return jnp.where(row == 0, scale_ref[0], jnp.where(row == 1, scale_ref[1], scale_ref[2]))
-
-
 def partials(full_width, *refs):
-    *stat_refs, scale_ref, hr_ref, coef_ref, dw_ref = refs
+    *stat_refs, table_ref, hr_ref, coef_ref, dw_ref = refs
     total = stat_refs[0][...]
     for ref in stat_refs[1:]:
         total = total + ref[...]
@@ -125,7 +157,7 @@
     square = dcoef[COLUMNS : COLUMNS + 1]
     inv_rms = lax.rsqrt(square / full_width + 1e-06)
     bent = jnp.tanh(inv_rms * lin)
-    scales = scales_of(scale_ref, bent.shape)
+    scales = table_ref[PAD:, 0:1]
     dpre = jnp.where(iota(bent.shape, 0) < COLUMNS, dcoef * scales * (1.0 - bent * bent), 0.0)
     dlin = dpre * inv_rms
     dsquare = -0.5 * inv_rms * inv_rms * inv_rms / full_width * jnp.sum(dpre * lin, axis=0, keepdims=True)
@@ -151,7 +183,7 @@
     ]
 
 
-def outputs(first, groups, finished, last, coef_ref, mix_ref, hr_ref, gr_ref, g0_ref, w_ref, *refs):
+def outputs(first, groups, finished, last, coef_ref, table_ref, hr_ref, gr_ref, g0_ref, w_ref, *refs):
     *results, grad_buf, out_buf, sems, more_sems = refs
     group, streams, width = grad_buf.shape[0] // groups, grad_buf.shape[1], grad_buf.shape[2]
     copies = put((*refs[:2], *results[-2:]), first * group - refs[1].shape[0], sems) if finished else []
@@ -168,11 +200,7 @@
     kept = kept | ((lane >= at_w) & (lane < at_h))
     out_token, out_lane = iota((group, end), 0), iota((group, end), 1)
     out_kept = (out_lane < at_g0) & (out_lane // streams == out_token)
-    row, stream = iota((PAD, rows), 0), iota((PAD, rows), 1) % streams
-    static = jnp.zeros((PAD, rows), F32)
-    for j in range(streams):
-        for c in range(COLUMNS):
-            static = jnp.where((row == c) & (stream == j), mix_ref[j, c], static)
+    static = table_ref[:PAD, :rows]
     lefts = []
     for index in range(groups):
         here = coef_ref[first + index]
@@ -228,7 +256,6 @@
     dp, tensor = lax.axis_size("dp"), lax.axis_size("tensor")
     full_width = width * tensor
     params = pltpu.CompilerParams(vmem_limit_bytes=VMEM_LIMIT)
-    scalars = pl.BlockSpec(memory_space=pltpu.SMEM)
 
     block = min(STAT_TOKENS, tokens)
     def in_hbm(array):
@@ -240,16 +267,17 @@
     streams, cotangent, layer_out, input_cot = map(in_hbm, (streams, cotangent, layer_out, input_cot))
     vmem = pl.BlockSpec(memory_space=pltpu.VMEM)
     hbm = pl.BlockSpec(memory_space=pltpu.HBM)
-    stat, hr, gr, g0, w = pl.pallas_call(
+    stat, hr, gr, g0, w, table = pl.pallas_call(
         statistics,
-        in_specs=[hbm] * 6,
-        out_specs=[vmem] * 5,
+        in_specs=[hbm] * 8,
+        out_specs=[vmem] * 6,
         out_shape=[
             pltpu.VMEM((2 * PAD, rows), F32),
             pltpu.VMEM((rows, width), BF16),
             pltpu.VMEM((rows, width), BF16),
             pltpu.VMEM((tokens, width), BF16),
             pltpu.VMEM((2 * PAD, width), BF16),
+            pltpu.VMEM((2 * PAD, 128), F32),
         ],
         scratch_shapes=[
             pltpu.VMEM(streams.shape, BF16),
@@ -257,12 +285,17 @@
             pltpu.VMEM(layer_out.shape, BF16),
             pltpu.VMEM((1, width), F32),
             pltpu.VMEM((COLUMNS, width), F32),
+            pltpu.VMEM(static_mix.shape, F32),
+            pltpu.VMEM((1, *tanh_scale.shape), F32),
             pltpu.SemaphoreType.DMA((tokens // block, 4)),
-            pltpu.SemaphoreType.DMA((2,)),
+            pltpu.SemaphoreType.DMA((4,)),
         ],
         compiler_params=params,
         name="statistics",
-    )(streams, cotangent, layer_out, input_cot, in_hbm(gain.reshape(1, width)), in_hbm(projection))
+    )(
+        *(streams, cotangent, layer_out, input_cot),
+        *map(in_hbm, (gain.reshape(1, width), projection, static_mix, tanh_scale.reshape(1, -1))),
+    )
 
     if tensor == 2:
         stats = (stat, lax.ppermute(stat, "tensor", [(0, 1), (1, 0)]))
@@ -272,7 +305,7 @@
     group = min(MIX_TOKENS, tokens)
     coef, dw = pl.pallas_call(
         lambda *refs: partials(float(full_width), *refs),
-        in_specs=[vmem] * len(stats) + [scalars, vmem],
+        in_specs=[vmem] * (len(stats) + 2),
         out_specs=[vmem] * 2,
         out_shape=[
             pltpu.VMEM((tokens // group, 3 * PAD, group * count), F32),
@@ -280,7 +313,7 @@
         ],
         compiler_params=params,
         name="partials",
-    )(*stats, tanh_scale, in_vmem(hr))
+    )(*stats, in_vmem(table), in_vmem(hr))
 
     grads = [jax.ShapeDtypeStruct((tokens, count, width), BF16), jax.ShapeDtypeStruct((tokens, width), BF16)]
 
@@ -291,7 +324,7 @@
         shape = (grads if bufs or last else []) + ([] if last else kept)
         done = pl.pallas_call(
             lambda *refs: outputs(first, groups, bool(bufs), last, *refs),
-            in_specs=[vmem, scalars] + [vmem] * (4 + len(bufs)) + [hbm] * len(results),
+            in_specs=[vmem] * (6 + len(bufs)) + [hbm] * len(results),
             out_specs=([hbm] * 2 if bufs or last else []) + ([] if last else [vmem] * 2),
             out_shape=shape,
             scratch_shapes=(kept if last else []) + sems,
@@ -299,7 +332,7 @@
             compiler_params=params,
             cost_estimate=pl.CostEstimate(flops=4_000_000_000, bytes_accessed=own * width * 30, transcendentals=0),
             name="outputs",
-        )(in_vmem(coef), static_mix, *map(in_vmem, (hr, gr, g0, w, *bufs)), *results)
+        )(*map(in_vmem, (coef, table)), *map(in_vmem, (hr, gr, g0, w, *bufs)), *results)
         return ((), done) if last else (done[-2:], done[:-2])
 
     sizes = [tokens // group]

time: 29.8 us -> 29.4 us (0.987)
  Pallas kernels: 15.1 us -> 12.3 us
  waiting for transfers between devices: 3.14 us -> 5.49 us
    ppermute x4, waiting for transfers between devices: 2.28 us -> 4.63 us  [shards(): more = lax.ppermute(dw, ('dp', 'tensor'), pairs)]
    pallas_call x4, Pallas kernels: 8.11 us -> 5.77 us  [mixed(): pl.pallas_call(lambda *refs: outputs(first, groups, bool(bufs), last, *re...]
    pallas_call x1, Pallas kernels: 1.19 us -> 0.69 us  [shards(): pl.pallas_call(lambda *refs: partials(float(full_width), *refs), in_specs...]
  transfers between devices with their start and end apart: 5 -> 5, of which waited for: 5 -> 5; matrix products, arithmetic and copies ran while one was open for 0% -> 0% of each run, Pallas kernels for 27% -> 20%
where the time goes in v4:
time: 29.4 us; the launch traced here: 29.3 us
  Pallas kernels  12.3 us (42%)
  starting transfers between devices  10.7 us (36%)
  waiting for transfers between devices  5.49 us (19%)
  between operations  0.69 us (2%)
    ppermute x4, starting transfers between devices, shards(): more = lax.ppermute(dw, ('dp', 'tensor'), pairs)  10.1 us
    pallas_call x4, Pallas kernels, mixed(): pl.pallas_call(lambda *refs: outputs(first, groups, bool(bufs), last, *re...  5.77 us
    pallas_call x1, Pallas kernels, shards(): pl.pallas_call(statistics, in_specs=[hbm] * 8, out_specs=[vmem] * 6, out_...  5.14 us
    ppermute x4, waiting for transfers between devices, shards(): more = lax.ppermute(dw, ('dp', 'tensor'), pairs)  4.63 us
    ppermute x1, waiting for transfers between devices, shards(): stats = (stat, lax.ppermute(stat, 'tensor', [(0, 1), (1, 0)]))  0.86 us
    pallas_call x1, Pallas kernels, shards(): pl.pallas_call(lambda *refs: tail(proj_scale, gain_scale, *refs), in_spec...  0.73 us
    pallas_call x1, Pallas kernels, shards(): pl.pallas_call(lambda *refs: partials(float(full_width), *refs), in_specs...  0.69 us
  transfers between devices with their start and end apart: 5, of which 5 were waited for; matrix products, arithmetic and copies ran while one was open for 0% of the time, Pallas kernels for 20%

profile of v4, /device:TPU:0, one launch (start us, length us, event | category | flops | bytes accessed | tf_op | source)
XLA Modules:
  0.0 29.3 jit_solution(308572466897415087)
XLA Ops:
  0.6 5.1 %statistics.1 = (f32[16,512]{1,0:T(8,128)S(1)}, bf16[512,4096]{1,0:T(8,128)(2,1)S(1)}, bf16[512,4096]{1,0:T(8,128)(2,1)S(1)}, bf16[128,4096]{1,0:T(8,128)(2,1)S(...) custom-call(bf16[128,4,4096]{2,1,0:T(4,128)(2,1)} %h_hbm.1, bf16[128,4,4096]{2,1,0:T(4,128)(2,1)} %g_hbm.1, ...), custom_call_target="tpu_custom_call" | custom-call | tf_op jit(solution)/shard_map/statistics/pallas_call | solution.py:270
  5.8 0.6 %collective-permute-start = (f32[16,512]{1,0:T(8,128)S(1)}, f32[16,512]{1,0:T(8,128)S(1)}, u32[]{:S(2)}, u32[]{:S(2)}) collective-permute-start(f32[16,512]{1,0:T(8,128)S(1)} %get-tuple-element.26.refs_0_), channel_id=1, source_target_pairs={{0,1},{1,0},{2,3},{3,2},{4,5},{5,4},{6,7},{7,6},{8,9},{9,8},{10,11... | collective-permute-start | bytes 98312 | tf_op jit(solution)/shard_map/ppermute | solution.py:301
  6.3 0.9 %collective-permute-done.refs_1_ = f32[16,512]{1,0:T(8,128)S(1)} collective-permute-done((f32[16,512]{1,0:T(8,128)S(1)}, f32[16,512]{1,0:T(8,128)S(1)}, u32[]{:S(2)}, u32[]{:S(2)}) %collective-permute-start) | collective-permute-done | bytes 32800 | tf_op jit(solution)/shard_map/ppermute | solution.py:301
  7.2 0.7 %partials.1 = (f32[8,24,64]{2,1,0:T(8,128)S(1)}, f32[24,1024]{1,0:T(8,128)S(1)}) custom-call(f32[16,512]{1,0:T(8,128)S(1)} %get-tuple-element.26.refs_0_, f32[16,512]{1,0:T(8,128)S(1)} %collective-permute-done.refs_1_, f32[16,128]{1,0:T(8,128)S(1)} %get-tuple-element.27.refs_2_.refs_1_, bf16[512,4096]{1,0:T(8,128)(2,1)S(1)} %get-tuple-element.28.refs_3_.refs_2_), custom_call_target="tpu_custom_call" | custom-call | tf_op jit(solution)/shard_map/partials/pallas_call | solution.py:306
  7.9 2.8 %collective-permute-start.1 = (f32[24,1024]{1,0:T(8,128)S(1)}, f32[24,1024]{1,0:T(8,128)S(1)}, u32[]{:S(2)}, u32[]{:S(2)}) collective-permute-start(f32[24,1024]{1,0:T(8,128)S(1)} %get-tuple-element.45), channel_id=1, source_target_pairs={{0,2},{1,9},{2,0},{3,11},{4,6},{5,13},{6,4},{7,15},{8,10},{9,1},{1... | collective-permute-start | bytes 294920 | tf_op jit(solution)/shard_map/ppermute | solution.py:354
  10.7 1.6 %outputs.4 = (bf16[48,4,4096]{2,1,0:T(4,128)(2,1)S(1)}, bf16[48,4096]{1,0:T(8,128)(2,1)S(1)}) custom-call(f32[8,24,64]{2,1,0:T(8,128)S(1)} %get-tuple-element.29.refs_0_, f32[16,128]{1,0:T(8,128)S(1)} %get-tuple-element.27.refs_2_.refs_1_, bf16[512,4096]{1,0:T(8,128)(2,1)S(1)} %get-tuple-element.28.refs_3_.refs_2_, ...), custom_call_target="tpu_custom_call" | custom-call | flops 4000000000 | bytes 5898240 | tf_op jit(solution)/shard_map/outputs/pallas_call | solution.py:325
  12.3 1.0 %collective-permute-done.1 = f32[24,1024]{1,0:T(8,128)S(1)} collective-permute-done((f32[24,1024]{1,0:T(8,128)S(1)}, f32[24,1024]{1,0:T(8,128)S(1)}, u32[]{:S(2)}, u32[]{:S(2)}) %collective-permute-start.1) | collective-permute-done | bytes 98336 | tf_op jit(solution)/shard_map/ppermute | solution.py:354
  13.3 2.2 %collective-permute-start.2 = (f32[24,1024]{1,0:T(8,128)S(1)}, f32[24,1024]{1,0:T(8,128)S(1)}, u32[]{:S(2)}, u32[]{:S(2)}) collective-permute-start(f32[24,1024]{1,0:T(8,128)S(1)} %add.9), channel_id=1, source_target_pairs={{0,8},{1,3},{2,10},{3,1},{4,12},{5,7},{6,14},{7,5},{8,0},{9,11},{1... | collective-permute-start | bytes 294920 | tf_op jit(solution)/shard_map/ppermute | solution.py:354
  15.5 1.3 %outputs.5 = (bf16[128,4,4096]{2,1,0:T(4,128)(2,1)}, bf16[128,4096]{1,0:T(8,128)(2,1)}, bf16[32,4,4096]{2,1,0:T(4,128)(2,1)S(1)}, bf16[32,4096]{1,0:T(8,128)(2,1)S(1)}) custom-call(f32[8,24,64]{2,1,0:T(8,128)S(1)} %get-tuple-element.29.refs_0_, f32[16,128]{1,0:T(8,128)S(1)} %get-tuple-element.27.refs_2_.refs_1_, ...), custom_call_target="tpu_custom_call" | custom-call | flops 4000000000 | bytes 3932160 | tf_op jit(solution)/shard_map/outputs/pallas_call | solution.py:325
  16.8 1.3 %collective-permute-done.2 = f32[24,1024]{1,0:T(8,128)S(1)} collective-permute-done((f32[24,1024]{1,0:T(8,128)S(1)}, f32[24,1024]{1,0:T(8,128)S(1)}, u32[]{:S(2)}, u32[]{:S(2)}) %collective-permute-start.2) | collective-permute-done | bytes 98336 | tf_op jit(solution)/shard_map/ppermute | solution.py:354
  18.1 2.0 %collective-permute-start.3 = (f32[24,1024]{1,0:T(8,128)S(1)}, f32[24,1024]{1,0:T(8,128)S(1)}, u32[]{:S(2)}, u32[]{:S(2)}) collective-permute-start(f32[24,1024]{1,0:T(8,128)S(1)} %add.10), channel_id=1, source_target_pairs={{0,4},{1,17},{2,6},{3,19},{4,0},{5,21},{6,2},{7,23},{8,12},{9,25},... | collective-permute-start | bytes 294920 | tf_op jit(solution)/shard_map/ppermute | solution.py:354
  20.2 1.2 %outputs.6 = (bf16[128,4,4096]{2,1,0:T(4,128)(2,1)}, bf16[128,4096]{1,0:T(8,128)(2,1)}, bf16[32,4,4096]{2,1,0:T(4,128)(2,1)S(1)}, bf16[32,4096]{1,0:T(8,128)(2,1)S(1)}) custom-call(f32[8,24,64]{2,1,0:T(8,128)S(1)} %get-tuple-element.29.refs_0_, f32[16,128]{1,0:T(8,128)S(1)} %get-tuple-element.27.refs_2_.refs_1_, ...), custom_call_target="tpu_custom_call", output_to_operand_aliasing={{0}: (8, {}), {1}: (9, {})} | custom-call | flops 4000000000 | bytes 3932160 | tf_op jit(solution)/shard_map/outputs/pallas_call | solution.py:325
  21.4 1.4 %collective-permute-done.3 = f32[24,1024]{1,0:T(8,128)S(1)} collective-permute-done((f32[24,1024]{1,0:T(8,128)S(1)}, f32[24,1024]{1,0:T(8,128)S(1)}, u32[]{:S(2)}, u32[]{:S(2)}) %collective-permute-start.3) | collective-permute-done | bytes 98336 | tf_op jit(solution)/shard_map/ppermute | solution.py:354
  22.8 3.1 %collective-permute-start.4 = (f32[24,1024]{1,0:T(8,128)S(1)}, f32[24,1024]{1,0:T(8,128)S(1)}, u32[]{:S(2)}, u32[]{:S(2)}) collective-permute-start(f32[24,1024]{1,0:T(8,128)S(1)} %add.11.refs_0_), channel_id=1, source_target_pairs={{0,16},{1,5},{2,18},{3,7},{4,20},{5,1},{6,22},{7,3},{8,24},{9,13},... | collective-permute-start | bytes 294920 | tf_op jit(solution)/shard_map/ppermute | solution.py:354
  25.9 0.0 copy-start
  25.9 0.0 copy-start.1
  25.9 1.7 %outputs.7 = (bf16[128,4,4096]{2,1,0:T(4,128)(2,1)}, bf16[128,4096]{1,0:T(8,128)(2,1)}) custom-call(f32[8,24,64]{2,1,0:T(8,128)S(1)} %get-tuple-element.29.refs_0_, f32[16,128]{1,0:T(8,128)S(1)} %get-tuple-element.27.refs_2_.refs_1_, bf16[512,4096]{1,0:T(8,128)(2,1)S(1)} %get-tuple-element.28.refs_3_.refs_2_, ...), custom_call_target="tpu_custom_call", output_to_operand_aliasing={{0}: (8, {}), {1}: (9, {})} | custom-call | flops 4000000000 | bytes 1966080 | tf_op jit(solution)/shard_map/outputs/pallas_call | solution.py:325
  27.6 0.9 %collective-permute-done.4.refs_1_ = f32[24,1024]{1,0:T(8,128)S(1)} collective-permute-done((f32[24,1024]{1,0:T(8,128)S(1)}, f32[24,1024]{1,0:T(8,128)S(1)}, u32[]{:S(2)}, u32[]{:S(2)}) %collective-permute-start.4) | collective-permute-done | bytes 98336 | tf_op jit(solution)/shard_map/ppermute | solution.py:354
  28.5 0.0 copy-done
  28.5 0.0 copy-done.1
  28.5 0.7 %tail.1 = (f32[6,4096]{1,0:T(8,128)}, f32[1,4096]{1,0:T(1,128)}) custom-call(f32[24,1024]{1,0:T(8,128)S(1)} %add.11.refs_0_, f32[24,1024]{1,0:T(8,128)S(1)} %collective-permute-done.4.refs_1_, f32[1,4096]{1,0:T(1,128)S(1)} %bitcast.4, f32[6,4096]{1,0:T(8,128)S(1)} %copy-done), custom_call_target="tpu_custom_call" | custom-call | tf_op jit(solution)/shard_map/tail/pallas_call | solution.py:362
  (3 shorter events, 0.0 us)
Async XLA Ops:
  5.8 1.4 %collective-permute-start = (f32[16,512]{1,0:T(8,128)S(1)}, f32[16,512]{1,0:T(8,128)S(1)}, u32[]{:S(2)}, u32[]{:S(2)}) collective-permute-start(f32[16,512]{1,0:T(8,128)S(1)} %get-tuple-element.26.refs_0_), channel_id=1, source_target_pairs={{0,1},{1,0},{2,3},{3,2},{4,5},{5,4},{6,7},{7,6},{8,9},{9,8},{10,11... | collective-permute-start | bytes 98312 | tf_op jit(solution)/shard_map/ppermute | solution.py:301
  7.9 5.4 %collective-permute-start.1 = (f32[24,1024]{1,0:T(8,128)S(1)}, f32[24,1024]{1,0:T(8,128)S(1)}, u32[]{:S(2)}, u32[]{:S(2)}) collective-permute-start(f32[24,1024]{1,0:T(8,128)S(1)} %get-tuple-element.45), channel_id=1, source_target_pairs={{0,2},{1,9},{2,0},{3,11},{4,6},{5,13},{6,4},{7,15},{8,10},{9,1},{1... | collective-permute-start | bytes 294920 | tf_op jit(solution)/shard_map/ppermute | solution.py:354
  13.3 4.8 %collective-permute-start.2 = (f32[24,1024]{1,0:T(8,128)S(1)}, f32[24,1024]{1,0:T(8,128)S(1)}, u32[]{:S(2)}, u32[]{:S(2)}) collective-permute-start(f32[24,1024]{1,0:T(8,128)S(1)} %add.9), channel_id=1, source_target_pairs={{0,8},{1,3},{2,10},{3,1},{4,12},{5,7},{6,14},{7,5},{8,0},{9,11},{1... | collective-permute-start | bytes 294920 | tf_op jit(solution)/shard_map/ppermute | solution.py:354
  18.1 4.7 %collective-permute-start.3 = (f32[24,1024]{1,0:T(8,128)S(1)}, f32[24,1024]{1,0:T(8,128)S(1)}, u32[]{:S(2)}, u32[]{:S(2)}) collective-permute-start(f32[24,1024]{1,0:T(8,128)S(1)} %add.10), channel_id=1, source_target_pairs={{0,4},{1,17},{2,6},{3,19},{4,0},{5,21},{6,2},{7,23},{8,12},{9,25},... | collective-permute-start | bytes 294920 | tf_op jit(solution)/shard_map/ppermute | solution.py:354
  22.8 5.7 %collective-permute-start.4 = (f32[24,1024]{1,0:T(8,128)S(1)}, f32[24,1024]{1,0:T(8,128)S(1)}, u32[]{:S(2)}, u32[]{:S(2)}) collective-permute-start(f32[24,1024]{1,0:T(8,128)S(1)} %add.11.refs_0_), channel_id=1, source_target_pairs={{0,16},{1,5},{2,18},{3,7},{4,20},{5,1},{6,22},{7,3},{8,24},{9,13},... | collective-permute-start | bytes 294920 | tf_op jit(solution)/shard_map/ppermute | solution.py:354
  25.9 2.6 %copy-start = (f32[6,4096]{1,0:T(8,128)S(1)}, f32[6,4096]{1,0:T(8,128)}, u32[]{:S(2)}) copy-start(f32[6,4096]{1,0:T(8,128)} %refs_3_.1) | copy-start | bytes 294916
  25.9 2.6 %copy-start.1 = (f32[4096]{0:T(1024)S(1)}, f32[4096]{0:T(1024)}, u32[]{:S(2)}) copy-start(f32[4096]{0:T(1024)} %param.12) | copy-start | bytes 49156
